TPU v7x, 32 devices: a whole 2x2x4 slice. The times are simulated.
32 devices in a mesh: groups: 2 (over y), tile: 4 (over z), tracer: 4 (over x, core).
Axes of the slice: x: 2, y: 2, z: 4, core: 2. Of those that a mesh axis runs over, the one named last changes fastest.
Arguments:
- species_amounts: float32 [64, 32, 128, 128], P(('groups', 'tracer'), None, 'tile'), parts along dimension 0, may hold values from 0.2 to 2
- face_currents: float32 [2, 64, 128, 128], P(None, 'groups', 'tile'), parts along dimension 1, may hold values from -1 to 1
- thermal_anomaly: float32 [64, 128, 128], P(('groups', 'tracer'), 'tile'), parts along dimension 0, may hold values from -4 to 4
- layer_total_per_profile: int32 [256, 128], P(('groups', 'tile')), parts along dimension 0, may hold values from 0 to 32
- consumed_species: int32 [32], replicated, may hold values from 0 to 31, each once
- attenuation_factor: float32 [32], replicated, may hold values from 0.009375 to 0.09375
- intake_speedup: float32 [32], replicated, may hold values from 0.3 to 3
- incoming_sunshine: float32 [256, 128], P(('groups', 'tile')), parts along dimension 0, may hold values from 0.5 to 2
Outputs:
- tracers_out: float32 [64, 32, 128, 128], P('groups', 'tracer', 'tile'), parts along dimension 0
- velocity_out: float32 [2, 64, 128, 128], P(None, ('groups', 'tracer'), 'tile'), parts along dimension 1
- temperature_out: float32 [64, 128, 128], P(('groups', 'tracer'), 'tile'), parts along dimension 0
There are 2 independent parts, one for each index of `groups`. A program takes and returns all parts, laid end to end along the dimension named above; an argument that names none is the same for every part. Nothing has to cross between parts.
Inputs may be any that keep to these rules, and one draw needn't show every extreme that they name: Levels 0 to layer_total_per_profile - 1 of a column are sea, deeper levels are land; 0 marks a land column. `consumed_species`: A permutation of the 32 tracers.
All inputs are finite; a program needn't handle non-finite values.
Results may differ from a plain program's by a relative error of at most 0.0003.
Values sent between devices are 32-bit elements; how exact they have to be, the bound alone decides.
A program may use at most 64 MiB of HBM per device.

v0:
```python
import functools

import jax
import jax.numpy as jnp
from jax import lax
from jax.experimental import pallas as pl
from jax.experimental.pallas import tpu as pltpu
from jax.sharding import PartitionSpec as P

MESH = pl.DeviceIdType.MESH

sub_step = 0.45
step_duration = 0.2
gravity = 0.5
viscosity = 0.2
coriolis_base = 0.5
beta_plane = 0.5
spreading_coefficient = 0.2
water_clear = 0.05
column_optical = 3.0
warming_coefficient = 5.0
light_half = 0.3
nutrient_half = 0.5

PAD = 8
EDGE = 4
TILE = 8


def lane_index(shape):
    return lax.broadcasted_iota(jnp.int32, shape, len(shape) - 1)


def east(x):
    return pltpu.roll(x, x.shape[0] - 1, 0)


def west(x):
    return pltpu.roll(x, 1, 0)


def north(x):
    return jnp.where(lane_index(x.shape) == x.shape[1] - 1, 0.0, pltpu.roll(x, x.shape[1] - 1, 1))


def south(x):
    return jnp.where(lane_index(x.shape) == 0, 0.0, pltpu.roll(x, 1, 1))


def minmod(a, b):
    return jnp.maximum(jnp.minimum(a, b), 0.0) + jnp.minimum(jnp.maximum(a, b), 0.0)


def laplacian(x):
    return east(x) + west(x) + north(x) + south(x) - 4.0 * x


def substep(c, es, ns, lane):
    last = c.shape[1] - 1
    d = east(c) - c
    half = 0.5 * minmod(west(d), d)
    flux = es * jnp.where(es > 0.0, c + half, east(c - half))
    spread = flux - west(flux)
    d = jnp.where(lane == last, 0.0, pltpu.roll(c, last, 1)) - c
    half = 0.5 * minmod(jnp.where(lane == 0, c, pltpu.roll(d, 1, 1)), d)
    flux = ns * jnp.where(ns > 0.0, c + half, pltpu.roll(c - half, last, 1))
    return c - (spread + (flux - pltpu.roll(flux, 1, 1)))


def react_level(count, level, depth, sun, tau, cells, c, eaten, eater, att, rate, scale, sat, pull, put):
    total = jnp.full(depth.shape, water_clear, jnp.float32)
    for t in range(count):
        x = cells[t, c]
        size = jnp.abs(x)
        total = total + att[t] * size
        sat[t] = x / (nutrient_half + size)
        pull[t] = rate[t] * x
    optical = total * scale
    wet = jnp.where(level < depth, 1.0, 0.0)
    caught = sun * jnp.exp(-tau) * (1.0 - jnp.exp(-optical))
    mean_light = caught / optical
    gain = wet * (mean_light / (mean_light + light_half))
    for t in range(count):
        change = pull[t] * sat[eaten[t]] - pull[eater[t]] * sat[t]
        put(t, cells[t, c] + gain * change)
    return wet, caught, tau + optical


def transport_kernel(
    tiles, ranks, cores, q,
    sp, fc, th, dep, sun, eaten, att, rate,
    cells, vel, heat, aux,
    ext, fext, hext, dext, adv, tot, pre, over, sat, pull, eater,
    h_send, h_recv, f_send, f_recv, s_send, s_recv,
    d_send, d_recv, i_send, i_recv, e_send, e_recv, o_send, o_recv,
    l_sem, lf_sem, ls_sem,
):
    nt, nl, rows, width = sp.shape
    per = nl // ranks
    nc = per // q
    count = ranks * nt
    chips = ranks // cores
    cross = ranks - cores
    full = rows + 2 * PAD
    r = lax.axis_index("tracer")
    z = lax.axis_index("tile")
    a, b = r // cores, lax.rem(r, cores)
    up, down = lax.rem(z + 1, tiles), lax.rem(z + tiles - 1, tiles)

    def target(s):
        ka, kb = lax.rem(1 + s // cores, chips), cores - 1 - lax.rem(s, cores)
        return lax.rem(a + ka, chips) * cores + lax.rem(b + kb, cores)

    def source(s):
        ka, kb = lax.rem(1 + s // cores, chips), cores - 1 - lax.rem(s, cores)
        return lax.rem(a + chips - ka, chips) * cores + lax.rem(b + cores - kb, cores)

    def first_level(s, c):
        return target(s) * per + c * q

    mine = pl.ds(r * nt, nt)
    low_rows = pl.ds(0, EDGE)
    high_rows = pl.ds(rows - EDGE, EDGE)
    from_low = pl.ds(PAD - EDGE, EDGE)
    from_high = pl.ds(PAD + rows, EDGE)
    body = pl.ds(PAD, rows)
    inner = pl.ds(TILE, rows - 2 * TILE)

    def pair(src, dst, lead, send, recv, at):
        return (
            pltpu.make_async_remote_copy(
                src.at[lead + (high_rows,)], dst.at[lead + (from_low,)],
                send.at[at + (0,)], recv.at[at + (0,)],
                device_id={"tile": up}, device_id_type=MESH,
            ),
            pltpu.make_async_remote_copy(
                src.at[lead + (low_rows,)], dst.at[lead + (from_high,)],
                send.at[at + (1,)], recv.at[at + (1,)],
                device_id={"tile": down}, device_id_type=MESH,
            ),
        )

    def edges(s, c):
        n = s * nc + c
        lead = (slice(None), pl.ds(first_level(s, c), q))
        return (
            pair(fc, fext, lead, f_send, f_recv, (n,))
            + pair(sp, ext, lead, h_send, h_recv, (n,))
        )

    def heat_edges():
        return pair(th, hext, (slice(None),), s_send, s_recv, (0,))

    def depth_edges():
        return pair(dep, dext, (), s_send, s_recv, (1,))

    def local(s, c):
        n = s * nc + c
        lev = pl.ds(first_level(s, c), q)
        return (
            pltpu.make_async_copy(fc.at[:, lev], fext.at[:, lev, body], lf_sem.at[n]),
            pltpu.make_async_copy(sp.at[:, lev], ext.at[:, lev, body], l_sem.at[n]),
        )

    def block_copy(s, c, rank):
        n = s * nc + c
        return pltpu.make_async_remote_copy(
            adv.at[:, pl.ds(first_level(s, c), q)],
            cells.at[pl.ds(rank * nt, nt), pl.ds(c * q, q)],
            d_send.at[n], d_recv.at[n],
            device_id={"tracer": target(s)}, device_id_type=MESH,
        )

    def inner_copy(s, i, rank):
        return pltpu.make_async_remote_copy(
            adv.at[:, first_level(s, 0) + i, inner],
            cells.at[pl.ds(rank * nt, nt), i, inner],
            i_send.at[s, i], i_recv.at[s, i],
            device_id={"tracer": target(s)}, device_id_type=MESH,
        )

    def outer_copy(s, side, rank):
        part = pl.ds(side * (rows - TILE), TILE)
        return pltpu.make_async_remote_copy(
            adv.at[:, pl.ds(first_level(s, 0), q), part],
            cells.at[pl.ds(rank * nt, nt), pl.ds(0, q), part],
            e_send.at[s, side], e_recv.at[s, side],
            device_id={"tracer": target(s)}, device_id_type=MESH,
        )

    def over_copy(s, place):
        return pltpu.make_async_remote_copy(
            pre.at[target(s)], over.at[place], o_send.at[s], o_recv.at[s],
            device_id={"tracer": target(s)}, device_id_type=MESH,
        )

    def in_cross(m):
        return lax.rem(m, cross), m // cross

    def in_near(m):
        return cross + m // nc, lax.rem(m, nc)

    barrier = pltpu.get_barrier_semaphore()
    for place in (up, down):
        pl.semaphore_signal(barrier, inc=1, device_id={"tile": place}, device_id_type=MESH)
    for s in range(ranks - 1):
        pl.semaphore_signal(barrier, inc=1, device_id={"tracer": target(s)}, device_id_type=MESH)

    dep_local = pltpu.make_async_copy(dep, dext.at[body], ls_sem.at[0])
    th_local = pltpu.make_async_copy(th, hext.at[:, body], ls_sem.at[1])
    sun_local = pltpu.make_async_copy(sun, aux.at[1], ls_sem.at[2])
    dep_local.start()

    def start_local(order):
        def step(m, carry):
            for copy in local(*order(m)):
                copy.start()
            return carry
        return step

    lax.fori_loop(0, cross * nc, start_local(in_cross), 0)
    lax.fori_loop(0, cores * nc, start_local(in_near), 0)
    th_local.start()
    sun_local.start()

    tot[...] = jnp.zeros_like(tot)
    dep_local.wait()

    def advect(lev, block, base, size, skip, first, keep, put):
        window = pl.ds(base, size)
        kept = pl.ds(first, keep)
        lane = lane_index((size, width))
        wet = jnp.where(lev < dext[window], 1.0, 0.0)
        es = sub_step * (fext[0, lev, window] * wet * east(wet))
        ns = sub_step * (fext[1, lev, window] * wet * north(wet))

        def one_tracer(t, acc):
            c = substep(ext[t, lev, window], es, ns, lane)
            c = substep(c, es, ns, lane)[skip:skip + keep]
            put(t, lev, kept, c)
            return acc + att[r * nt + t] * jnp.abs(c)

        tot[block, kept] = lax.fori_loop(0, nt, one_tracer, tot[block, kept], unroll=True)

    def put_adv(t, lev, kept, c):
        adv[t, lev, kept] = c

    def put_cells(t, lev, kept, c):
        cells[r * nt + t, lev - r * per, kept] = c

    def advance_inner(s, i):
        lev = first_level(s, 0) + i
        advect(lev, target(s), PAD, rows, TILE, TILE, rows - 2 * TILE, put_adv)

    def advance_outer(s, i, side):
        lev = first_level(s, 0) + i
        base = pl.multiple_of(side * (rows - PAD), TILE)
        first = pl.multiple_of(side * (rows - TILE), TILE)
        advect(lev, target(s), base, TILE + 2 * PAD, PAD, first, TILE, put_adv)

    def wait_local(s, c):
        for copy in local(s, c):
            copy.wait()

    def advance(s, c, put):
        wait_local(s, c)
        for copy in edges(s, c):
            copy.wait_recv()
        block = target(s)
        level_0 = first_level(s, c)

        def one_level(i, carry):
            advect(level_0 + i, block, 0, full, PAD, 0, rows, put)
            return carry

        lax.fori_loop(0, q, one_level, 0)

    def start_edges(order):
        def step(m, carry):
            for copy in edges(*order(m)):
                copy.start()
            return carry
        return step

    def inner_step(m, carry):
        s, i = m // q, lax.rem(m, q)

        @pl.when(i == 0)
        def _():
            wait_local(s, 0)

        advance_inner(s, i)

        @pl.when(m == 0)
        def _():
            pl.semaphore_wait(barrier, 2 + ranks - 1)
            for copy in depth_edges():
                copy.start()

        inner_copy(s, i, r).start()

        @pl.when(m == 0)
        def _():
            lax.fori_loop(0, cross, start_edges(in_cross), 0)

        return carry

    lax.fori_loop(0, cross * q, inner_step, 0)
    lax.fori_loop(cross, cross * nc, start_edges(in_cross), 0)
    lax.fori_loop(0, cores * nc, start_edges(in_near), 0)
    for copy in heat_edges():
        copy.start()
    for copy in depth_edges():
        copy.wait()

    def outer_step(s, carry):
        for copy in edges(s, 0):
            copy.wait_recv()

        def part(m, carry):
            advance_outer(s, lax.rem(m, q), m // q)
            return carry

        lax.fori_loop(0, 2 * q, part, 0)
        for side in range(2):
            outer_copy(s, side, r).start()
        return carry

    lax.fori_loop(0, cross, outer_step, 0)

    def away_step(m, carry):
        far = m < cross * nc
        k = m - cross * nc
        s = jnp.where(far, lax.rem(m, cross), cross + k // nc)
        c = jnp.where(far, m // cross, lax.rem(k, nc))
        advance(s, c, put_adv)

        @pl.when(jnp.logical_or(jnp.logical_not(far), c < nc - 1))
        def _():
            block_copy(s, c, r).start()

        return carry

    lax.fori_loop(cross, (ranks - 1) * nc, away_step, 0)

    def own_step(c, carry):
        advance(ranks - 1, c, put_cells)
        return carry

    lax.fori_loop(0, nc, own_step, 0)

    above = jnp.zeros((rows, width), jnp.float32)
    for place in range(ranks):
        pre[place] = above
        above = above + tot[place]
    for s in range(ranks - 1):
        over_copy(s, r).start()

    def late_step(s, carry):
        block_copy(s, nc - 1, r).start()
        return carry

    lax.fori_loop(0, cross, late_step, 0)

    th_local.wait()
    sun_local.wait()
    for copy in heat_edges():
        copy.wait()
    lane = lane_index((full, width))
    coriolis = coriolis_base + beta_plane * lane.astype(jnp.float32) / width

    def momentum(i, carry):
        lev = r * per + i
        u, v, heat_ext = fext[0, lev], fext[1, lev], hext[i]
        wet = jnp.where(lev < dext[...], 1.0, 0.0)
        v_east, u_west = east(v), west(u)
        v_bar = 0.25 * (v + v_east + south(v) + south(v_east))
        u_bar = 0.25 * (u + u_west + north(u) + north(u_west))
        new_u = u + step_duration * (
            coriolis * v_bar - gravity * (east(heat_ext) - heat_ext) + viscosity * laplacian(u)
        )
        new_v = v + step_duration * (
            -coriolis * u_bar - gravity * (north(heat_ext) - heat_ext) + viscosity * laplacian(v)
        )
        vel[0, i] = (wet * east(wet) * new_u)[PAD:PAD + rows]
        vel[1, i] = (wet * north(wet) * new_v)[PAD:PAD + rows]
        warmer = heat_ext + step_duration * spreading_coefficient * laplacian(heat_ext)
        heat[i] = warmer[PAD:PAD + rows]
        return carry

    lax.fori_loop(0, per, momentum, 0)

    def invert(s, carry):
        who = jnp.int32(0)
        for t in range(count):
            who = jnp.where(eaten[t] == s, jnp.int32(t), who)
        eater[s] = who
        return carry

    lax.fori_loop(0, count, invert, 0)

    depth = dext[PAD:PAD + rows].astype(jnp.float32)
    aux[2] = depth
    scale = column_optical / nl
    above = pre[r]
    for s in range(ranks - 1):
        over_copy(s, source(s)).wait_recv()
        above = above + over[source(s)]
    aux[0] = (above + (r * per).astype(jnp.float32) * water_clear) * scale

    def wait_far(c):
        def step(s, carry):
            block_copy(s, c, source(s)).wait_recv()
            return carry
        return step

    def react_chunk(c, carry):
        @pl.when(c == 0)
        def _():
            for s in range(cross):
                for i in range(q):
                    inner_copy(s, i, source(s)).wait_recv()
                for side in range(2):
                    outer_copy(s, side, source(s)).wait_recv()
            lax.fori_loop(cross, ranks - 1, wait_far(0), 0)

        @pl.when(c > 0)
        def _():
            lax.fori_loop(0, ranks - 1, wait_far(c), 0)

        def one_level(j, carry):
            i = c * q + j

            def put(t, x):
                cells[t, i] = x

            level = (r * per + i).astype(jnp.float32)
            wet, caught, below = react_level(
                count, level, aux[2], aux[1], aux[0], cells, i,
                eaten, eater, att, rate, scale, sat, pull, put,
            )
            aux[0] = below
            heat[i] = wet * (heat[i] + warming_coefficient * (caught * wet))
            return carry

        lax.fori_loop(0, q, one_level, 0)
        return carry

    lax.fori_loop(0, nc - 1, react_chunk, 0)

    def drain_edges(m, carry):
        for copy in edges(m // nc, lax.rem(m, nc)):
            copy.wait_send()
        return carry

    lax.fori_loop(0, ranks * nc, drain_edges, 0)
    for s in range(ranks - 1):
        over_copy(s, r).wait_send()
    for s in range(cross):
        for i in range(q):
            inner_copy(s, i, r).wait_send()
        for side in range(2):
            outer_copy(s, side, r).wait_send()

    def drain_far(m, carry):
        block_copy(lax.rem(m, cross), m // cross, r).wait_send()
        return carry

    lax.fori_loop(cross, cross * nc, drain_far, 0)

    def drain_near(m, carry):
        block_copy(cross + m // nc, lax.rem(m, nc), r).wait_send()
        return carry

    lax.fori_loop(0, (cores - 1) * nc, drain_near, 0)
    lax.fori_loop(0, ranks - 1, wait_far(nc - 1), 0)


def finish_kernel(
    levels, q,
    cells, vel, heat, aux, eaten, att, rate,
    out, vel_out, temp_out,
    last, warm, sat, pull, eater, sem, last_sem,
):
    count, per = cells.shape[:2]
    r = lax.axis_index("tracer")
    done = per - q
    scale = column_optical / levels
    copies = [
        pltpu.make_async_copy(cells.at[:, pl.ds(0, done)], out.at[:, pl.ds(0, done)], sem.at[0]),
        pltpu.make_async_copy(vel, vel_out, sem.at[1]),
        pltpu.make_async_copy(heat.at[pl.ds(0, done)], temp_out.at[pl.ds(0, done)], sem.at[2]),
    ]
    for copy in copies:
        copy.start()
    for t in range(count):
        eater[eaten[t]] = t

    def level_copy(j):
        return pltpu.make_async_copy(last.at[j], out.at[:, done + j], last_sem.at[j])

    def one_level(j, tau):
        def put(t, x):
            last[j, t] = x

        level = (r * per + done + j).astype(jnp.float32)
        wet, caught, below = react_level(
            count, level, aux[2], aux[1], tau, cells, done + j,
            eaten, eater, att, rate, scale, sat, pull, put,
        )
        warm[j] = wet * (heat[done + j] + warming_coefficient * (caught * wet))
        level_copy(j).start()
        return below

    lax.fori_loop(0, q, one_level, aux[0])
    warm_copy = pltpu.make_async_copy(warm, temp_out.at[pl.ds(done, q)], sem.at[3])
    warm_copy.start()
    for copy in copies:
        copy.wait()
    for j in range(q):
        level_copy(j).wait()
    warm_copy.wait()


def solution(mesh):
    tiles, ranks = mesh.shape["tile"], mesh.shape["tracer"]
    cores = 2 if ranks % 2 == 0 else 1

    def on_device(
        species_amounts,
        face_currents,
        thermal_anomaly,
        layer_total_per_profile,
        consumed_species,
        attenuation_factor,
        intake_speedup,
        incoming_sunshine,
    ):
        nt, nl, rows, width = species_amounts.shape
        per = nl // ranks
        q = 2 if per % 2 == 0 else 1
        chunks = nl // q
        count = ranks * nt
        cross = ranks - cores
        full = rows + 2 * PAD
        f32 = jnp.float32
        any_space = pl.BlockSpec(memory_space=pl.ANY)
        vmem = pl.BlockSpec(memory_space=pltpu.VMEM)
        smem = pl.BlockSpec(memory_space=pltpu.SMEM)
        dma = pltpu.SemaphoreType.DMA
        cells, vel, heat, aux = pl.pallas_call(
            functools.partial(transport_kernel, tiles, ranks, cores, q),
            out_shape=(
                pltpu.VMEM((count, per, rows, width), f32),
                pltpu.VMEM((2, per, rows, width), f32),
                pltpu.VMEM((per, rows, width), f32),
                pltpu.VMEM((3, rows, width), f32),
            ),
            in_specs=[any_space] * 5 + [smem] * 3,
            out_specs=(vmem, vmem, vmem, vmem),
            scratch_shapes=[
                pltpu.VMEM((nt, nl, full, width), f32),
                pltpu.VMEM((2, nl, full, width), f32),
                pltpu.VMEM((per, full, width), f32),
                pltpu.VMEM((full, width), jnp.int32),
                pltpu.VMEM((nt, nl, rows, width), f32),
                pltpu.VMEM((ranks, rows, width), f32),
                pltpu.VMEM((ranks, rows, width), f32),
                pltpu.VMEM((ranks, rows, width), f32),
                pltpu.VMEM((count, rows, width), f32),
                pltpu.VMEM((count, rows, width), f32),
                pltpu.SMEM((count,), jnp.int32),
                dma((chunks, 2)), dma((chunks, 2)),
                dma((chunks, 2)), dma((chunks, 2)),
                dma((2, 2)), dma((2, 2)),
                dma((chunks,)), dma((chunks,)),
                dma((cross, q)), dma((cross, q)),
                dma((cross, 2)), dma((cross, 2)),
                dma((ranks,)), dma((ranks,)),
                dma((chunks,)), dma((chunks,)), dma((3,)),
            ],
            compiler_params=pltpu.CompilerParams(
                collective_id=0, has_side_effects=True, vmem_limit_bytes=48 << 20
            ),
            name="transport",
        )(
            species_amounts, face_currents, thermal_anomaly,
            layer_total_per_profile, incoming_sunshine,
            consumed_species, attenuation_factor, intake_speedup,
        )
        return pl.pallas_call(
            functools.partial(finish_kernel, nl, q),
            out_shape=(
                jax.ShapeDtypeStruct((count, per, rows, width), f32),
                jax.ShapeDtypeStruct((2, per, rows, width), f32),
                jax.ShapeDtypeStruct((per, rows, width), f32),
            ),
            in_specs=[vmem] * 4 + [smem] * 3,
            out_specs=(any_space, any_space, any_space),
            scratch_shapes=[
                pltpu.VMEM((q, count, rows, width), f32),
                pltpu.VMEM((q, rows, width), f32),
                pltpu.VMEM((count, rows, width), f32),
                pltpu.VMEM((count, rows, width), f32),
                pltpu.SMEM((count,), jnp.int32),
                dma((4,)), dma((q,)),
            ],
            compiler_params=pltpu.CompilerParams(vmem_limit_bytes=32 << 20),
            name="finish",
        )(
            cells, vel, heat, aux,
            consumed_species, attenuation_factor, intake_speedup,
        )

    return jax.shard_map(
        on_device,
        mesh=mesh,
        in_specs=(
            P(("groups", "tracer"), None, "tile", None),
            P(None, "groups", "tile", None),
            P(("groups", "tracer"), "tile", None),
            P(("groups", "tile"), None),
            P(),
            P(),
            P(),
            P(("groups", "tile"), None),
        ),
        out_specs=(
            P("groups", "tracer", "tile", None),
            P(None, ("groups", "tracer"), "tile", None),
            P(("groups", "tracer"), "tile", None),
        ),
        check_vma=False,
    )
```

profile of v0, /device:TPU:0, one launch (start us, length us, event | category | flops | bytes accessed | tf_op | source)
XLA Modules:
  0.0 65.0 jit_solution(766490840704427245)
XLA Ops:
  0.6 0.0 copy-start
  0.6 1.2 %copy-done = f32[2,32,32,128]{3,2,1,0:T(8,128)S(1)} copy-done((f32[2,32,32,128]{3,2,1,0:T(8,128)S(1)}, f32[2,32,32,128]{3,2,1,0:T(8,128)}, u32[]{:S(2)}) %copy-start) | copy-done | bytes 1048600
  1.9 0.0 copy-start.1
  1.9 0.9 %copy-done.1 = f32[8,32,128]{2,1,0:T(8,128)S(1)} copy-done((f32[8,32,128]{2,1,0:T(8,128)S(1)}, f32[8,32,128]{2,1,0:T(8,128)}, u32[]{:S(2)}) %copy-start.1) | copy-done | bytes 131096
  2.8 0.0 copy-start.2
  2.8 0.7 %copy-done.2 = s32[32,128]{1,0:T(8,128)S(1)} copy-done((s32[32,128]{1,0:T(8,128)S(1)}, s32[32,128]{1,0:T(8,128)}, u32[]{:S(2)}) %copy-start.2) | copy-done | bytes 16408
  3.5 0.0 copy-start.3
  3.5 0.7 %copy-done.3 = f32[32,128]{1,0:T(8,128)S(1)} copy-done((f32[32,128]{1,0:T(8,128)S(1)}, f32[32,128]{1,0:T(8,128)}, u32[]{:S(2)}) %copy-start.3) | copy-done | bytes 16408
  4.2 0.0 copy-start.4
  4.2 0.7 %copy-done.4 = s32[32]{0:T(128)S(1)} copy-done((s32[32]{0:T(128)S(1)}, s32[32]{0:T(128)}, u32[]{:S(2)}) %copy-start.4) | copy-done | bytes 152
  4.9 0.0 copy-start.5
  4.9 0.7 %copy-done.5 = f32[32]{0:T(128)S(1)} copy-done((f32[32]{0:T(128)S(1)}, f32[32]{0:T(128)}, u32[]{:S(2)}) %copy-start.5) | copy-done | bytes 152
  5.5 0.0 copy-start.6
  5.5 0.7 %copy-done.6 = f32[32]{0:T(128)S(1)} copy-done((f32[32]{0:T(128)S(1)}, f32[32]{0:T(128)}, u32[]{:S(2)}) %copy-start.6) | copy-done | bytes 152
  6.2 56.1 %transport.1 = (f32[32,8,32,128]{3,2,1,0:T(8,128)S(1)}, f32[2,8,32,128]{3,2,1,0:T(8,128)S(1)}, f32[8,32,128]{2,1,0:T(8,128)S(1)}, f32[3,32,128]{2,1,0:T(8,128)S(1)}) custom-call(f32[8,32,32,128]{3,2,1,0:T(8,128)} %sp.1, f32[2,32,32,128]{3,2,1,0:T(8,128)S(1)} %copy-done, f32[8,32,128]{2,1,0:T(8,128)S(1)} %copy-done.1, s32[32,128]{1,0:T(8,128)S(1)} %copy-done.2, ...), custom_call_target="tpu_custom_call" | custom-call | tf_op jit(solution)/shard_map/transport/pallas_call | solution.py:551
  62.3 2.7 %finish.1 = (f32[32,8,32,128]{3,2,1,0:T(8,128)}, f32[2,8,32,128]{3,2,1,0:T(8,128)}, f32[8,32,128]{2,1,0:T(8,128)}) custom-call(f32[32,8,32,128]{3,2,1,0:T(8,128)S(1)} %get-tuple-element.7.cells, f32[2,8,32,128]{3,2,1,0:T(8,128)S(1)} %get-tuple-element.8.vel, f32[8,32,128]{2,1,0:T(8,128)S(1)} %get-tuple-element.9.heat, ...), custom_call_target="tpu_custom_call" | custom-call | tf_op jit(solution)/shard_map/finish/pallas_call | solution.py:591
Async XLA Ops:
  0.6 1.2 %copy-start = (f32[2,32,32,128]{3,2,1,0:T(8,128)S(1)}, f32[2,32,32,128]{3,2,1,0:T(8,128)}, u32[]{:S(2)}) copy-start(f32[2,32,32,128]{3,2,1,0:T(8,128)} %fc.1) | copy-start | bytes 3145732
  1.9 0.9 %copy-start.1 = (f32[8,32,128]{2,1,0:T(8,128)S(1)}, f32[8,32,128]{2,1,0:T(8,128)}, u32[]{:S(2)}) copy-start(f32[8,32,128]{2,1,0:T(8,128)} %th.1) | copy-start | bytes 393220
  2.8 0.7 %copy-start.2 = (s32[32,128]{1,0:T(8,128)S(1)}, s32[32,128]{1,0:T(8,128)}, u32[]{:S(2)}) copy-start(s32[32,128]{1,0:T(8,128)} %dep.1) | copy-start | bytes 49156
  3.5 0.7 %copy-start.3 = (f32[32,128]{1,0:T(8,128)S(1)}, f32[32,128]{1,0:T(8,128)}, u32[]{:S(2)}) copy-start(f32[32,128]{1,0:T(8,128)} %sun.1) | copy-start | bytes 49156
  4.2 0.7 %copy-start.4 = (s32[32]{0:T(128)S(1)}, s32[32]{0:T(128)}, u32[]{:S(2)}) copy-start(s32[32]{0:T(128)} %eaten.3) | copy-start | bytes 388
  4.9 0.7 %copy-start.5 = (f32[32]{0:T(128)S(1)}, f32[32]{0:T(128)}, u32[]{:S(2)}) copy-start(f32[32]{0:T(128)} %att.3) | copy-start | bytes 388
  5.5 0.7 %copy-start.6 = (f32[32]{0:T(128)S(1)}, f32[32]{0:T(128)}, u32[]{:S(2)}) copy-start(f32[32]{0:T(128)} %rate.3) | copy-start | bytes 388
where the time goes:
time: 65.3 us; the launch traced here: 65 us
  Pallas kernels  58.8 us (90%)
  local copies, waits for them, and re-layouts  5.52 us (8%)
  between operations  0.66 us (1%)
    pallas_call x1, Pallas kernels, on_device(): pl.pallas_call(functools.partial(transport_kernel, tiles, ranks, cores, q...  56.1 us
    unnamed x14, local copies, waits for them, and re-layouts  5.52 us
    pallas_call x1, Pallas kernels, on_device(): pl.pallas_call(functools.partial(finish_kernel, nl, q), out_shape=(jax.Sh...  2.73 us

commit v1 on v0

--- a/solution.py
+++ b/solution.py
@@ -25,6 +25,8 @@
 PAD = 8
 EDGE = 4
 TILE = 8
+
+HBM = pltpu.HBM
 
 
 def lane_index(shape):
@@ -88,12 +90,12 @@
 
 def transport_kernel(
     tiles, ranks, cores, q,
-    sp, fc, th, dep, sun, eaten, att, rate,
+    sp, fc, th, dep, sun, eaten_in, att_in, rate_in,
     cells, vel, heat, aux,
-    ext, fext, hext, dext, adv, tot, pre, over, sat, pull, eater,
+    eaten, att, rate, ext, fext, hext, dext, adv, tot, pre, over, sat, pull, eater,
     h_send, h_recv, f_send, f_recv, s_send, s_recv,
     d_send, d_recv, i_send, i_recv, e_send, e_recv, o_send, o_recv,
-    l_sem, lf_sem, ls_sem,
+    l_sem, lf_sem, ls_sem, t_sem,
 ):
     nt, nl, rows, width = sp.shape
     per = nl // ranks
@@ -124,7 +126,7 @@
     from_low = pl.ds(PAD - EDGE, EDGE)
     from_high = pl.ds(PAD + rows, EDGE)
     body = pl.ds(PAD, rows)
-    inner = pl.ds(TILE, rows - 2 * TILE)
+    inner = pl.ds(EDGE, rows - 2 * EDGE)
 
     def pair(src, dst, lead, send, recv, at):
         return (
@@ -180,7 +182,7 @@
         )
 
     def outer_copy(s, side, rank):
-        part = pl.ds(side * (rows - TILE), TILE)
+        part = pl.ds(side * (rows - EDGE), EDGE)
         return pltpu.make_async_remote_copy(
             adv.at[:, pl.ds(first_level(s, 0), q), part],
             cells.at[pl.ds(rank * nt, nt), pl.ds(0, q), part],
@@ -209,7 +211,12 @@
     dep_local = pltpu.make_async_copy(dep, dext.at[body], ls_sem.at[0])
     th_local = pltpu.make_async_copy(th, hext.at[:, body], ls_sem.at[1])
     sun_local = pltpu.make_async_copy(sun, aux.at[1], ls_sem.at[2])
+    tables = [
+        pltpu.make_async_copy(src, dst, t_sem.at[k])
+        for k, (src, dst) in enumerate(((eaten_in, eaten), (att_in, att), (rate_in, rate)))
+    ]
     dep_local.start()
+    tables[1].start()
 
     def start_local(order):
         def step(m, carry):
@@ -222,9 +229,12 @@
     lax.fori_loop(0, cores * nc, start_local(in_near), 0)
     th_local.start()
     sun_local.start()
+    tables[0].start()
+    tables[2].start()
 
     tot[...] = jnp.zeros_like(tot)
     dep_local.wait()
+    tables[1].wait()
 
     def advect(lev, block, base, size, skip, first, keep, put):
         window = pl.ds(base, size)
@@ -250,13 +260,13 @@
 
     def advance_inner(s, i):
         lev = first_level(s, 0) + i
-        advect(lev, target(s), PAD, rows, TILE, TILE, rows - 2 * TILE, put_adv)
+        advect(lev, target(s), PAD, rows, EDGE, EDGE, rows - 2 * EDGE, put_adv)
 
     def advance_outer(s, i, side):
         lev = first_level(s, 0) + i
-        base = pl.multiple_of(side * (rows - PAD), TILE)
-        first = pl.multiple_of(side * (rows - TILE), TILE)
-        advect(lev, target(s), base, TILE + 2 * PAD, PAD, first, TILE, put_adv)
+        base = side * (rows - PAD)
+        skip, first = (TILE + EDGE, rows - EDGE) if side else (PAD, 0)
+        advect(lev, target(s), base, TILE + 2 * PAD, skip, first, EDGE, put_adv)
 
     def wait_local(s, c):
         for copy in local(s, c):
@@ -317,11 +327,12 @@
         for copy in edges(s, 0):
             copy.wait_recv()
 
-        def part(m, carry):
-            advance_outer(s, lax.rem(m, q), m // q)
+        def part(i, carry):
+            for side in range(2):
+                advance_outer(s, i, side)
             return carry
 
-        lax.fori_loop(0, 2 * q, part, 0)
+        lax.fori_loop(0, q, part, 0)
         for side in range(2):
             outer_copy(s, side, r).start()
         return carry
@@ -335,7 +346,7 @@
         c = jnp.where(far, m // cross, lax.rem(k, nc))
         advance(s, c, put_adv)
 
-        @pl.when(jnp.logical_or(jnp.logical_not(far), c < nc - 1))
+        @pl.when(m != cross * nc - 1)
         def _():
             block_copy(s, c, r).start()
 
@@ -356,11 +367,7 @@
     for s in range(ranks - 1):
         over_copy(s, r).start()
 
-    def late_step(s, carry):
-        block_copy(s, nc - 1, r).start()
-        return carry
-
-    lax.fori_loop(0, cross, late_step, 0)
+    block_copy(cross - 1, nc - 1, r).start()
 
     th_local.wait()
     sun_local.wait()
@@ -389,6 +396,9 @@
         return carry
 
     lax.fori_loop(0, per, momentum, 0)
+
+    tables[0].wait()
+    tables[2].wait()
 
     def invert(s, carry):
         who = jnp.int32(0)
@@ -556,9 +566,12 @@
                 pltpu.VMEM((per, rows, width), f32),
                 pltpu.VMEM((3, rows, width), f32),
             ),
-            in_specs=[any_space] * 5 + [smem] * 3,
+            in_specs=[any_space] * 8,
             out_specs=(vmem, vmem, vmem, vmem),
             scratch_shapes=[
+                pltpu.SMEM((count,), jnp.int32),
+                pltpu.SMEM((count,), f32),
+                pltpu.SMEM((count,), f32),
                 pltpu.VMEM((nt, nl, full, width), f32),
                 pltpu.VMEM((2, nl, full, width), f32),
                 pltpu.VMEM((per, full, width), f32),
@@ -577,16 +590,18 @@
                 dma((cross, q)), dma((cross, q)),
                 dma((cross, 2)), dma((cross, 2)),
                 dma((ranks,)), dma((ranks,)),
-                dma((chunks,)), dma((chunks,)), dma((3,)),
+                dma((chunks,)), dma((chunks,)), dma((3,)), dma((3,)),
             ],
             compiler_params=pltpu.CompilerParams(
                 collective_id=0, has_side_effects=True, vmem_limit_bytes=48 << 20
             ),
             name="transport",
         )(
-            species_amounts, face_currents, thermal_anomaly,
-            layer_total_per_profile, incoming_sunshine,
-            consumed_species, attenuation_factor, intake_speedup,
+            *(pltpu.with_memory_space_constraint(x, HBM) for x in (
+                species_amounts, face_currents, thermal_anomaly,
+                layer_total_per_profile, incoming_sunshine,
+                consumed_species, attenuation_factor, intake_speedup,
+            ))
         )
         return pl.pallas_call(
             functools.partial(finish_kernel, nl, q),

time: 65.3 us -> 58.3 us (0.89)
  local copies, waits for them, and re-layouts: 5.52 us -> 0.01 us
  Pallas kernels: 58.8 us -> 57.5 us
    unnamed x14 -> x6, local copies, waits for them, and re-layouts: 5.52 us -> 0.01 us
    pallas_call x1, Pallas kernels: 56.1 us -> 54.7 us  [on_device(): pl.pallas_call(functools.partial(transport_kernel, tiles, ranks, cores, q...]
where the time goes in v1:
time: 58.3 us; the launch traced here: 58.2 us
  Pallas kernels  57.5 us (99%)
  between operations  0.69 us (1%)
    pallas_call x1, Pallas kernels, on_device(): pl.pallas_call(functools.partial(transport_kernel, tiles, ranks, cores, q...  54.7 us
    pallas_call x1, Pallas kernels, on_device(): pl.pallas_call(functools.partial(finish_kernel, nl, q), out_shape=(jax.Sh...  2.73 us

profile of v1, /device:TPU:0, one launch (start us, length us, event | category | flops | bytes accessed | tf_op | source)
XLA Modules:
  0.0 58.2 jit_solution(12152394721376345375)
XLA Ops:
  0.6 0.0 copy-start.2
  0.6 0.0 copy-start.1
  0.7 0.0 copy-start
  0.7 54.7 %transport.1 = (f32[32,8,32,128]{3,2,1,0:T(8,128)S(1)}, f32[2,8,32,128]{3,2,1,0:T(8,128)S(1)}, f32[8,32,128]{2,1,0:T(8,128)S(1)}, f32[3,32,128]{2,1,0:T(8,128)S(1)}) custom-call(f32[8,32,32,128]{3,2,1,0:T(8,128)} %sp.1, f32[2,32,32,128]{3,2,1,0:T(8,128)} %fc.1, f32[8,32,128]{2,1,0:T(8,128)} %th.1, s32[32,128]{1,0:T(8,128)} %dep.1, f32[32,128]{1,0:T(8,128)} %sun.1, ...), custom_call_target="tpu_custom_call" | custom-call | tf_op jit(solution)/shard_map/transport/pallas_call | solution.py:561
  55.4 0.0 copy-done.2
  55.4 0.0 copy-done.1
  55.4 0.0 copy-done
  55.4 2.7 %finish.1 = (f32[32,8,32,128]{3,2,1,0:T(8,128)}, f32[2,8,32,128]{3,2,1,0:T(8,128)}, f32[8,32,128]{2,1,0:T(8,128)}) custom-call(f32[32,8,32,128]{3,2,1,0:T(8,128)S(1)} %get-tuple-element.7.cells, f32[2,8,32,128]{3,2,1,0:T(8,128)S(1)} %get-tuple-element.8.vel, f32[8,32,128]{2,1,0:T(8,128)S(1)} %get-tuple-element.9.heat, ...), custom_call_target="tpu_custom_call" | custom-call | tf_op jit(solution)/shard_map/finish/pallas_call | solution.py:606
Async XLA Ops:
  0.6 54.8 %copy-start.2 = (f32[32]{0:T(128)S(1)}, f32[32]{0:T(128)}, u32[]{:S(2)}) copy-start(f32[32]{0:T(128)} %rate.1) | copy-start | bytes 388
  0.6 54.8 %copy-start.1 = (f32[32]{0:T(128)S(1)}, f32[32]{0:T(128)}, u32[]{:S(2)}) copy-start(f32[32]{0:T(128)} %att.1) | copy-start | bytes 388
  0.7 54.8 %copy-start = (s32[32]{0:T(128)S(1)}, s32[32]{0:T(128)}, u32[]{:S(2)}) copy-start(s32[32]{0:T(128)} %eaten.1) | copy-start | bytes 388

commit v2 on v1

--- a/solution.py
+++ b/solution.py
@@ -25,6 +25,7 @@
 PAD = 8
 EDGE = 4
 TILE = 8
+LOW_FLOW, HIGH_FLOW = 3, 2
 
 HBM = pltpu.HBM
 
@@ -89,13 +90,13 @@
 
 
 def transport_kernel(
-    tiles, ranks, cores, q,
+    tiles, ranks, cores, q, early,
     sp, fc, th, dep, sun, eaten_in, att_in, rate_in,
     cells, vel, heat, aux,
-    eaten, att, rate, ext, fext, hext, dext, adv, tot, pre, over, sat, pull, eater,
+    eaten, att, rate, ext, fext, hext, dext, adv, tot, pre, part, joined, over, sat, pull, eater,
     h_send, h_recv, f_send, f_recv, s_send, s_recv,
-    d_send, d_recv, i_send, i_recv, e_send, e_recv, o_send, o_recv,
-    l_sem, lf_sem, ls_sem, t_sem,
+    d_send, d_recv, i_send, i_recv, e_send, e_recv, o_send, o_recv, p_send, p_recv,
+    l_sem, lf_sem, ls_sem, t_sem, ready,
 ):
     nt, nl, rows, width = sp.shape
     per = nl // ranks
@@ -121,22 +122,20 @@
         return target(s) * per + c * q
 
     mine = pl.ds(r * nt, nt)
-    low_rows = pl.ds(0, EDGE)
-    high_rows = pl.ds(rows - EDGE, EDGE)
-    from_low = pl.ds(PAD - EDGE, EDGE)
-    from_high = pl.ds(PAD + rows, EDGE)
     body = pl.ds(PAD, rows)
     inner = pl.ds(EDGE, rows - 2 * EDGE)
 
-    def pair(src, dst, lead, send, recv, at):
+    def pair(src, dst, lead, send, recv, at, low=EDGE, high=EDGE):
         return (
             pltpu.make_async_remote_copy(
-                src.at[lead + (high_rows,)], dst.at[lead + (from_low,)],
+                src.at[lead + (pl.ds(rows - low, low),)],
+                dst.at[lead + (pl.ds(PAD - low, low),)],
                 send.at[at + (0,)], recv.at[at + (0,)],
                 device_id={"tile": up}, device_id_type=MESH,
             ),
             pltpu.make_async_remote_copy(
-                src.at[lead + (low_rows,)], dst.at[lead + (from_high,)],
+                src.at[lead + (pl.ds(0, high),)],
+                dst.at[lead + (pl.ds(PAD + rows, high),)],
                 send.at[at + (1,)], recv.at[at + (1,)],
                 device_id={"tile": down}, device_id_type=MESH,
             ),
@@ -146,7 +145,7 @@
         n = s * nc + c
         lead = (slice(None), pl.ds(first_level(s, c), q))
         return (
-            pair(fc, fext, lead, f_send, f_recv, (n,))
+            pair(fc, fext, lead, f_send, f_recv, (n,), LOW_FLOW, HIGH_FLOW)
             + pair(sp, ext, lead, h_send, h_recv, (n,))
         )
 
@@ -173,28 +172,40 @@
             device_id={"tracer": target(s)}, device_id_type=MESH,
         )
 
-    def inner_copy(s, i, rank):
+    def inner_copy(s, c, i, rank):
         return pltpu.make_async_remote_copy(
-            adv.at[:, first_level(s, 0) + i, inner],
-            cells.at[pl.ds(rank * nt, nt), i, inner],
-            i_send.at[s, i], i_recv.at[s, i],
+            adv.at[:, first_level(s, c) + i, inner],
+            cells.at[pl.ds(rank * nt, nt), c * q + i, inner],
+            i_send.at[c, s, i], i_recv.at[c, s, i],
             device_id={"tracer": target(s)}, device_id_type=MESH,
         )
 
-    def outer_copy(s, side, rank):
-        part = pl.ds(side * (rows - EDGE), EDGE)
+    def outer_copy(s, c, side, rank):
+        edge = pl.ds(side * (rows - EDGE), EDGE)
         return pltpu.make_async_remote_copy(
-            adv.at[:, pl.ds(first_level(s, 0), q), part],
-            cells.at[pl.ds(rank * nt, nt), pl.ds(0, q), part],
-            e_send.at[s, side], e_recv.at[s, side],
+            adv.at[:, pl.ds(first_level(s, c), q), edge],
+            cells.at[pl.ds(rank * nt, nt), pl.ds(c * q, q), edge],
+            e_send.at[c, s, side], e_recv.at[c, s, side],
             device_id={"tracer": target(s)}, device_id_type=MESH,
         )
 
-    def over_copy(s, place):
+    partner = a * cores + cores - 1 - b
+
+    def part_copy():
         return pltpu.make_async_remote_copy(
-            pre.at[target(s)], over.at[place], o_send.at[s], o_recv.at[s],
-            device_id={"tracer": target(s)}, device_id_type=MESH,
-        )
+            pre.at[:, cores - 1 - b], part, p_send.at[0], p_recv.at[0],
+            device_id={"tracer": partner}, device_id_type=MESH,
+        )
+
+    def over_copy(k):
+        there = lax.rem(a + k, chips)
+        return pltpu.make_async_remote_copy(
+            joined.at[there], over.at[k - 1], o_send.at[k - 1], o_recv.at[k - 1],
+            device_id={"tracer": there * cores + b}, device_id_type=MESH,
+        )
+
+    def gets_over(k):
+        return lax.rem(a + k, chips) * cores + b > 0
 
     def in_cross(m):
         return lax.rem(m, cross), m // cross
@@ -202,11 +213,19 @@
     def in_near(m):
         return cross + m // nc, lax.rem(m, nc)
 
+    last_core = a * cores + cores - 1
+    late = b == cores - 1
     barrier = pltpu.get_barrier_semaphore()
+    for s in range(cross):
+        pl.semaphore_signal(barrier, inc=1, device_id={"tracer": target(s)}, device_id_type=MESH)
+    if cores > 1:
+        @pl.when(jnp.logical_not(late))
+        def _():
+            pl.semaphore_signal(barrier, inc=1, device_id={"tracer": last_core}, device_id_type=MESH)
     for place in (up, down):
-        pl.semaphore_signal(barrier, inc=1, device_id={"tile": place}, device_id_type=MESH)
-    for s in range(ranks - 1):
-        pl.semaphore_signal(barrier, inc=1, device_id={"tracer": target(s)}, device_id_type=MESH)
+        pl.semaphore_signal(
+            barrier, inc=1, device_id={"tile": place, "tracer": last_core}, device_id_type=MESH
+        )
 
     dep_local = pltpu.make_async_copy(dep, dext.at[body], ls_sem.at[0])
     th_local = pltpu.make_async_copy(th, hext.at[:, body], ls_sem.at[1])
@@ -225,12 +244,7 @@
             return carry
         return step
 
-    lax.fori_loop(0, cross * nc, start_local(in_cross), 0)
-    lax.fori_loop(0, cores * nc, start_local(in_near), 0)
-    th_local.start()
-    sun_local.start()
-    tables[0].start()
-    tables[2].start()
+    lax.fori_loop(0, early * cross, start_local(in_cross), 0)
 
     tot[...] = jnp.zeros_like(tot)
     dep_local.wait()
@@ -258,12 +272,12 @@
     def put_cells(t, lev, kept, c):
         cells[r * nt + t, lev - r * per, kept] = c
 
-    def advance_inner(s, i):
-        lev = first_level(s, 0) + i
+    def advance_inner(s, c, i):
+        lev = first_level(s, c) + i
         advect(lev, target(s), PAD, rows, EDGE, EDGE, rows - 2 * EDGE, put_adv)
 
-    def advance_outer(s, i, side):
-        lev = first_level(s, 0) + i
+    def advance_outer(s, c, i, side):
+        lev = first_level(s, c) + i
         base = side * (rows - PAD)
         skip, first = (TILE + EDGE, rows - EDGE) if side else (PAD, 0)
         advect(lev, target(s), base, TILE + 2 * PAD, skip, first, EDGE, put_adv)
@@ -292,52 +306,73 @@
             return carry
         return step
 
+    turn = jnp.where(late, 0, min(early * cross * q, cross * q + q) - 1)
+
     def inner_step(m, carry):
-        s, i = m // q, lax.rem(m, q)
+        k, i = m // q, lax.rem(m, q)
+        s, c = in_cross(k)
 
         @pl.when(i == 0)
         def _():
-            wait_local(s, 0)
-
-        advance_inner(s, i)
+            wait_local(s, c)
+
+        advance_inner(s, c, i)
 
         @pl.when(m == 0)
         def _():
-            pl.semaphore_wait(barrier, 2 + ranks - 1)
+            pl.semaphore_wait(barrier, jnp.where(late, cross + cores - 1 + 2 * cores, cross))
+
+        inner_copy(s, c, i, r).start()
+
+        @pl.when(m == turn)
+        def _():
+            if cores > 1:
+                @pl.when(late)
+                def _():
+                    pl.semaphore_signal(
+                        ready, inc=1, device_id={"tracer": partner}, device_id_type=MESH
+                    )
+
+                @pl.when(jnp.logical_not(late))
+                def _():
+                    pl.semaphore_wait(ready, 1)
+
             for copy in depth_edges():
                 copy.start()
-
-        inner_copy(s, i, r).start()
-
-        @pl.when(m == 0)
-        def _():
             lax.fori_loop(0, cross, start_edges(in_cross), 0)
 
         return carry
 
-    lax.fori_loop(0, cross * q, inner_step, 0)
+    lax.fori_loop(0, early * cross * q, inner_step, 0)
     lax.fori_loop(cross, cross * nc, start_edges(in_cross), 0)
+    lax.fori_loop(early * cross, cross * nc, start_local(in_cross), 0)
     lax.fori_loop(0, cores * nc, start_edges(in_near), 0)
+    lax.fori_loop(0, cores * nc, start_local(in_near), 0)
     for copy in heat_edges():
         copy.start()
+    th_local.start()
+    sun_local.start()
+    tables[0].start()
+    tables[2].start()
     for copy in depth_edges():
         copy.wait()
 
-    def outer_step(s, carry):
-        for copy in edges(s, 0):
+    def outer_step(k, carry):
+        s, c = in_cross(k)
+        for copy in edges(s, c):
             copy.wait_recv()
 
-        def part(i, carry):
+        def sides(i, carry):
             for side in range(2):
-                advance_outer(s, i, side)
+                advance_outer(s, c, i, side)
             return carry
 
-        lax.fori_loop(0, q, part, 0)
+        lax.fori_loop(0, q, sides, 0)
         for side in range(2):
-            outer_copy(s, side, r).start()
-        return carry
-
-    lax.fori_loop(0, cross, outer_step, 0)
+            outer_copy(s, c, side, r).start()
+        return carry
+
+    lax.fori_loop(0, early * cross, outer_step, 0)
 
     def away_step(m, carry):
         far = m < cross * nc
@@ -352,7 +387,7 @@
 
         return carry
 
-    lax.fori_loop(cross, (ranks - 1) * nc, away_step, 0)
+    lax.fori_loop(early * cross, (ranks - 1) * nc, away_step, 0)
 
     def own_step(c, carry):
         advance(ranks - 1, c, put_cells)
@@ -362,10 +397,20 @@
 
     above = jnp.zeros((rows, width), jnp.float32)
     for place in range(ranks):
-        pre[place] = above
+        pre[place // cores, place % cores] = above
         above = above + tot[place]
-    for s in range(ranks - 1):
-        over_copy(s, r).start()
+    if cores > 1:
+        part_copy().start()
+        part_copy().wait()
+        for k in range(chips):
+            joined[k] = pre[k, b] + part[k]
+    else:
+        for k in range(chips):
+            joined[k] = pre[k, b]
+    for k in range(1, chips):
+        @pl.when(gets_over(k))
+        def _():
+            over_copy(k).start()
 
     block_copy(cross - 1, nc - 1, r).start()
 
@@ -412,11 +457,19 @@
     depth = dext[PAD:PAD + rows].astype(jnp.float32)
     aux[2] = depth
     scale = column_optical / nl
-    above = pre[r]
-    for s in range(ranks - 1):
-        over_copy(s, source(s)).wait_recv()
-        above = above + over[source(s)]
-    aux[0] = (above + (r * per).astype(jnp.float32) * water_clear) * scale
+    clear = (r * per).astype(jnp.float32) * water_clear
+
+    @pl.when(r == 0)
+    def _():
+        aux[0] = jnp.zeros((rows, width), jnp.float32)
+
+    @pl.when(r > 0)
+    def _():
+        above = joined[a]
+        for k in range(1, chips):
+            over_copy(k).wait_recv()
+            above = above + over[k - 1]
+        aux[0] = (above + clear) * scale
 
     def wait_far(c):
         def step(s, carry):
@@ -425,16 +478,19 @@
         return step
 
     def react_chunk(c, carry):
-        @pl.when(c == 0)
-        def _():
-            for s in range(cross):
+        @pl.when(c < early)
+        def _():
+            def first_parts(s, carry):
                 for i in range(q):
-                    inner_copy(s, i, source(s)).wait_recv()
+                    inner_copy(s, c, i, source(s)).wait_recv()
                 for side in range(2):
-                    outer_copy(s, side, source(s)).wait_recv()
-            lax.fori_loop(cross, ranks - 1, wait_far(0), 0)
-
-        @pl.when(c > 0)
+                    outer_copy(s, c, side, source(s)).wait_recv()
+                return carry
+
+            lax.fori_loop(0, cross, first_parts, 0)
+            lax.fori_loop(cross, ranks - 1, wait_far(c), 0)
+
+        @pl.when(c >= early)
         def _():
             lax.fori_loop(0, ranks - 1, wait_far(c), 0)
 
@@ -464,19 +520,27 @@
         return carry
 
     lax.fori_loop(0, ranks * nc, drain_edges, 0)
-    for s in range(ranks - 1):
-        over_copy(s, r).wait_send()
-    for s in range(cross):
+    for k in range(1, chips):
+        @pl.when(gets_over(k))
+        def _():
+            over_copy(k).wait_send()
+
+    def drain_first(k, carry):
+        s, c = in_cross(k)
         for i in range(q):
-            inner_copy(s, i, r).wait_send()
+            inner_copy(s, c, i, r).wait_send()
         for side in range(2):
-            outer_copy(s, side, r).wait_send()
+            outer_copy(s, c, side, r).wait_send()
+        return carry
+
+    lax.fori_loop(0, early * cross, drain_first, 0)
 
     def drain_far(m, carry):
-        block_copy(lax.rem(m, cross), m // cross, r).wait_send()
-        return carry
-
-    lax.fori_loop(cross, cross * nc, drain_far, 0)
+        s, c = in_cross(m)
+        block_copy(s, c, r).wait_send()
+        return carry
+
+    lax.fori_loop(early * cross, cross * nc, drain_far, 0)
 
     def drain_near(m, carry):
         block_copy(cross + m // nc, lax.rem(m, nc), r).wait_send()
@@ -552,6 +616,8 @@
         chunks = nl // q
         count = ranks * nt
         cross = ranks - cores
+        chips = ranks // cores
+        early = min(2, per // q - 1)
         full = rows + 2 * PAD
         f32 = jnp.float32
         any_space = pl.BlockSpec(memory_space=pl.ANY)
@@ -559,7 +625,7 @@
         smem = pl.BlockSpec(memory_space=pltpu.SMEM)
         dma = pltpu.SemaphoreType.DMA
         cells, vel, heat, aux = pl.pallas_call(
-            functools.partial(transport_kernel, tiles, ranks, cores, q),
+            functools.partial(transport_kernel, tiles, ranks, cores, q, early),
             out_shape=(
                 pltpu.VMEM((count, per, rows, width), f32),
                 pltpu.VMEM((2, per, rows, width), f32),
@@ -578,8 +644,10 @@
                 pltpu.VMEM((full, width), jnp.int32),
                 pltpu.VMEM((nt, nl, rows, width), f32),
                 pltpu.VMEM((ranks, rows, width), f32),
-                pltpu.VMEM((ranks, rows, width), f32),
-                pltpu.VMEM((ranks, rows, width), f32),
+                pltpu.VMEM((chips, cores, rows, width), f32),
+                pltpu.VMEM((chips, rows, width), f32),
+                pltpu.VMEM((chips, rows, width), f32),
+                pltpu.VMEM((chips, rows, width), f32),
                 pltpu.VMEM((count, rows, width), f32),
                 pltpu.VMEM((count, rows, width), f32),
                 pltpu.SMEM((count,), jnp.int32),
@@ -587,10 +655,11 @@
                 dma((chunks, 2)), dma((chunks, 2)),
                 dma((2, 2)), dma((2, 2)),
                 dma((chunks,)), dma((chunks,)),
-                dma((cross, q)), dma((cross, q)),
-                dma((cross, 2)), dma((cross, 2)),
-                dma((ranks,)), dma((ranks,)),
+                dma((early, cross, q)), dma((early, cross, q)),
+                dma((early, cross, 2)), dma((early, cross, 2)),
+                dma((chips,)), dma((chips,)), dma((1,)), dma((1,)),
                 dma((chunks,)), dma((chunks,)), dma((3,)), dma((3,)),
+                pltpu.SemaphoreType.REGULAR,
             ],
             compiler_params=pltpu.CompilerParams(
                 collective_id=0, has_side_effects=True, vmem_limit_bytes=48 << 20

time: 58.3 us -> 56.5 us (0.969); the launches traced: 58.2 us -> 55.5 us
  Pallas kernels: 57.5 us -> 54.8 us
    pallas_call x1, Pallas kernels: 54.7 us -> 52 us  [on_device(): pl.pallas_call(functools.partial(transport_kernel, tiles, ranks, cores, q...]
where the time goes in v2:
time: 56.5 us; the launch traced here: 55.5 us
  Pallas kernels  54.8 us (97%)
  between operations  0.69 us (1%)
    pallas_call x1, Pallas kernels, on_device(): pl.pallas_call(functools.partial(transport_kernel, tiles, ranks, cores, q...  52 us
    pallas_call x1, Pallas kernels, on_device(): pl.pallas_call(functools.partial(finish_kernel, nl, q), out_shape=(jax.Sh...  2.73 us

profile of v2, /device:TPU:0, one launch (start us, length us, event | category | flops | bytes accessed | tf_op | source)
XLA Modules:
  0.0 55.5 jit_solution(4230234006910541420)
XLA Ops:
  0.6 0.0 copy-start.2
  0.6 0.0 copy-start.1
  0.7 0.0 copy-start
  0.7 52.0 %transport.1 = (f32[32,8,32,128]{3,2,1,0:T(8,128)S(1)}, f32[2,8,32,128]{3,2,1,0:T(8,128)S(1)}, f32[8,32,128]{2,1,0:T(8,128)S(1)}, f32[3,32,128]{2,1,0:T(8,128)S(1)}) custom-call(f32[8,32,32,128]{3,2,1,0:T(8,128)} %sp.1, f32[2,32,32,128]{3,2,1,0:T(8,128)} %fc.1, f32[8,32,128]{2,1,0:T(8,128)} %th.1, s32[32,128]{1,0:T(8,128)} %dep.1, f32[32,128]{1,0:T(8,128)} %sun.1, ...), custom_call_target="tpu_custom_call" | custom-call | tf_op jit(solution)/shard_map/transport/pallas_call | solution.py:627
  52.7 0.0 copy-done.2
  52.7 0.0 copy-done.1
  52.7 0.0 copy-done
  52.7 2.7 %finish.1 = (f32[32,8,32,128]{3,2,1,0:T(8,128)}, f32[2,8,32,128]{3,2,1,0:T(8,128)}, f32[8,32,128]{2,1,0:T(8,128)}) custom-call(f32[32,8,32,128]{3,2,1,0:T(8,128)S(1)} %get-tuple-element.7.cells, f32[2,8,32,128]{3,2,1,0:T(8,128)S(1)} %get-tuple-element.8.vel, f32[8,32,128]{2,1,0:T(8,128)S(1)} %get-tuple-element.9.heat, ...), custom_call_target="tpu_custom_call" | custom-call | tf_op jit(solution)/shard_map/finish/pallas_call | solution.py:675
Async XLA Ops:
  0.6 52.1 %copy-start.2 = (f32[32]{0:T(128)S(1)}, f32[32]{0:T(128)}, u32[]{:S(2)}) copy-start(f32[32]{0:T(128)} %rate.1) | copy-start | bytes 388
  0.6 52.1 %copy-start.1 = (f32[32]{0:T(128)S(1)}, f32[32]{0:T(128)}, u32[]{:S(2)}) copy-start(f32[32]{0:T(128)} %att.1) | copy-start | bytes 388
  0.7 52.1 %copy-start = (s32[32]{0:T(128)S(1)}, s32[32]{0:T(128)}, u32[]{:S(2)}) copy-start(s32[32]{0:T(128)} %eaten.1) | copy-start | bytes 388

commit v3 on v2

--- a/solution.py
+++ b/solution.py
@@ -94,8 +94,7 @@
     sp, fc, th, dep, sun, eaten_in, att_in, rate_in,
     cells, vel, heat, aux,
     eaten, att, rate, ext, fext, hext, dext, adv, tot, pre, part, joined, over, sat, pull, eater,
-    h_send, h_recv, f_send, f_recv, s_send, s_recv,
-    d_send, d_recv, i_send, i_recv, e_send, e_recv, o_send, o_recv, p_send, p_recv,
+    edge_send, h_recv, f_recv, s_recv, d_send, d_recv, o_send, o_recv,
     l_sem, lf_sem, ls_sem, t_sem, ready,
 ):
     nt, nl, rows, width = sp.shape
@@ -110,13 +109,13 @@
     a, b = r // cores, lax.rem(r, cores)
     up, down = lax.rem(z + 1, tiles), lax.rem(z + tiles - 1, tiles)
 
+    def steps(s):
+        k = lax.rem(s, cores)
+        return lax.rem(1 + s // cores, chips), jnp.where(s < cross, k, cores - 1 - k)
+
     def target(s):
-        ka, kb = lax.rem(1 + s // cores, chips), cores - 1 - lax.rem(s, cores)
+        ka, kb = steps(s)
         return lax.rem(a + ka, chips) * cores + lax.rem(b + kb, cores)
-
-    def source(s):
-        ka, kb = lax.rem(1 + s // cores, chips), cores - 1 - lax.rem(s, cores)
-        return lax.rem(a + chips - ka, chips) * cores + lax.rem(b + cores - kb, cores)
 
     def first_level(s, c):
         return target(s) * per + c * q
@@ -125,82 +124,95 @@
     body = pl.ds(PAD, rows)
     inner = pl.ds(EDGE, rows - 2 * EDGE)
 
-    def pair(src, dst, lead, send, recv, at, low=EDGE, high=EDGE):
+    def settle(ref, sem):
+        pltpu.make_async_copy(ref, ref, sem).wait()
+
+    def pair(src, dst, lead, send, recv, low=EDGE, high=EDGE):
         return (
             pltpu.make_async_remote_copy(
                 src.at[lead + (pl.ds(rows - low, low),)],
                 dst.at[lead + (pl.ds(PAD - low, low),)],
-                send.at[at + (0,)], recv.at[at + (0,)],
-                device_id={"tile": up}, device_id_type=MESH,
+                send, recv, device_id={"tile": up}, device_id_type=MESH,
             ),
             pltpu.make_async_remote_copy(
                 src.at[lead + (pl.ds(0, high),)],
                 dst.at[lead + (pl.ds(PAD + rows, high),)],
-                send.at[at + (1,)], recv.at[at + (1,)],
-                device_id={"tile": down}, device_id_type=MESH,
+                send, recv, device_id={"tile": down}, device_id_type=MESH,
             ),
         )
 
     def edges(s, c):
-        n = s * nc + c
+        g = jnp.where(s < cross, c, nc + s - cross)
         lead = (slice(None), pl.ds(first_level(s, c), q))
         return (
-            pair(fc, fext, lead, f_send, f_recv, (n,), LOW_FLOW, HIGH_FLOW)
-            + pair(sp, ext, lead, h_send, h_recv, (n,))
-        )
+            pair(fc, fext, lead, edge_send.at[0], f_recv.at[g], LOW_FLOW, HIGH_FLOW)
+            + pair(sp, ext, lead, edge_send.at[1], h_recv.at[g])
+        )
+
+    def wait_edges(g, levels):
+        settle(fext.at[:, pl.ds(0, levels), pl.ds(0, LOW_FLOW + HIGH_FLOW)], f_recv.at[g])
+        settle(ext.at[:, pl.ds(0, levels), pl.ds(0, 2 * EDGE)], h_recv.at[g])
 
     def heat_edges():
-        return pair(th, hext, (slice(None),), s_send, s_recv, (0,))
+        return pair(th, hext, (slice(None),), edge_send.at[2], s_recv.at[0])
 
     def depth_edges():
-        return pair(dep, dext, (), s_send, s_recv, (1,))
-
-    def local(s, c):
-        n = s * nc + c
-        lev = pl.ds(first_level(s, c), q)
-        return (
-            pltpu.make_async_copy(fc.at[:, lev], fext.at[:, lev, body], lf_sem.at[n]),
-            pltpu.make_async_copy(sp.at[:, lev], ext.at[:, lev, body], l_sem.at[n]),
-        )
-
-    def block_copy(s, c, rank):
-        n = s * nc + c
+        return pair(dep, dext, (), edge_send.at[3], s_recv.at[1])
+
+    def flow_local(s):
+        lev = pl.ds(target(s) * per, per)
+        sem = lf_sem.at[0] if s == 0 else lf_sem.at[1]
+        return pltpu.make_async_copy(fc.at[:, lev], fext.at[:, lev, body], sem)
+
+    def early_local(k):
+        lev = pl.ds(first_level(k // early, lax.rem(k, early)), q)
+        return pltpu.make_async_copy(sp.at[:, lev], ext.at[:, lev, body], l_sem.at[k])
+
+    def rest_local(s):
+        skip = early if s < cross else 0
+        lev = pl.ds(first_level(s, skip), per - skip * q)
+        return pltpu.make_async_copy(sp.at[:, lev], ext.at[:, lev, body], l_sem.at[early * cross])
+
+    def block_copy(s, c):
         return pltpu.make_async_remote_copy(
             adv.at[:, pl.ds(first_level(s, c), q)],
-            cells.at[pl.ds(rank * nt, nt), pl.ds(c * q, q)],
-            d_send.at[n], d_recv.at[n],
+            cells.at[mine, pl.ds(c * q, q)],
+            d_send.at[0], d_recv.at[c],
             device_id={"tracer": target(s)}, device_id_type=MESH,
         )
 
-    def inner_copy(s, c, i, rank):
+    def inner_copy(s, c, i):
         return pltpu.make_async_remote_copy(
             adv.at[:, first_level(s, c) + i, inner],
-            cells.at[pl.ds(rank * nt, nt), c * q + i, inner],
-            i_send.at[c, s, i], i_recv.at[c, s, i],
+            cells.at[mine, c * q + i, inner],
+            d_send.at[0], d_recv.at[c],
             device_id={"tracer": target(s)}, device_id_type=MESH,
         )
 
-    def outer_copy(s, c, side, rank):
+    def outer_copy(s, c, side):
         edge = pl.ds(side * (rows - EDGE), EDGE)
         return pltpu.make_async_remote_copy(
             adv.at[:, pl.ds(first_level(s, c), q), edge],
-            cells.at[pl.ds(rank * nt, nt), pl.ds(c * q, q), edge],
-            e_send.at[c, s, side], e_recv.at[c, s, side],
+            cells.at[mine, pl.ds(c * q, q), edge],
+            d_send.at[0], d_recv.at[c],
             device_id={"tracer": target(s)}, device_id_type=MESH,
         )
+
+    def wait_blocks(c):
+        settle(cells.at[pl.ds(0, (ranks - 1) * nt), pl.ds(c * q, q)], d_recv.at[c])
 
     partner = a * cores + cores - 1 - b
 
     def part_copy():
         return pltpu.make_async_remote_copy(
-            pre.at[:, cores - 1 - b], part, p_send.at[0], p_recv.at[0],
+            pre.at[:, cores - 1 - b], part, o_send.at[0], o_recv.at[0],
             device_id={"tracer": partner}, device_id_type=MESH,
         )
 
     def over_copy(k):
         there = lax.rem(a + k, chips)
         return pltpu.make_async_remote_copy(
-            joined.at[there], over.at[k - 1], o_send.at[k - 1], o_recv.at[k - 1],
+            joined.at[there], over.at[k - 1], o_send.at[k], o_recv.at[k],
             device_id={"tracer": there * cores + b}, device_id_type=MESH,
         )
 
@@ -216,11 +228,15 @@
     last_core = a * cores + cores - 1
     late = b == cores - 1
     barrier = pltpu.get_barrier_semaphore()
-    for s in range(cross):
+    for s in range(0, cross, cores):
         pl.semaphore_signal(barrier, inc=1, device_id={"tracer": target(s)}, device_id_type=MESH)
     if cores > 1:
         @pl.when(jnp.logical_not(late))
         def _():
+            for s in range(1, cross, cores):
+                pl.semaphore_signal(
+                    barrier, inc=1, device_id={"tracer": target(s)}, device_id_type=MESH
+                )
             pl.semaphore_signal(barrier, inc=1, device_id={"tracer": last_core}, device_id_type=MESH)
     for place in (up, down):
         pl.semaphore_signal(
@@ -237,14 +253,15 @@
     dep_local.start()
     tables[1].start()
 
-    def start_local(order):
-        def step(m, carry):
-            for copy in local(*order(m)):
-                copy.start()
-            return carry
-        return step
-
-    lax.fori_loop(0, early * cross, start_local(in_cross), 0)
+    flow_local(0).start()
+
+    def start_early(k, carry):
+        early_local(k).start()
+        return carry
+
+    lax.fori_loop(0, early * cross, start_early, 0)
+    for s in range(1, ranks):
+        flow_local(s).start()
 
     tot[...] = jnp.zeros_like(tot)
     dep_local.wait()
@@ -282,14 +299,7 @@
         skip, first = (TILE + EDGE, rows - EDGE) if side else (PAD, 0)
         advect(lev, target(s), base, TILE + 2 * PAD, skip, first, EDGE, put_adv)
 
-    def wait_local(s, c):
-        for copy in local(s, c):
-            copy.wait()
-
     def advance(s, c, put):
-        wait_local(s, c)
-        for copy in edges(s, c):
-            copy.wait_recv()
         block = target(s)
         level_0 = first_level(s, c)
 
@@ -306,23 +316,31 @@
             return carry
         return step
 
-    turn = jnp.where(late, 0, min(early * cross * q, cross * q + q) - 1)
+    turn = jnp.where(late, 0, early * q - 1)
 
     def inner_step(m, carry):
         k, i = m // q, lax.rem(m, q)
-        s, c = in_cross(k)
+        s, c = k // early, lax.rem(k, early)
+
+        @pl.when(m == 0)
+        def _():
+            flow_local(0).wait()
+
+        @pl.when(m == early * q)
+        def _():
+            settle(fext.at[:, pl.ds(0, (ranks - 1) * per), body], lf_sem.at[1])
 
         @pl.when(i == 0)
         def _():
-            wait_local(s, c)
+            early_local(k).wait()
 
         advance_inner(s, c, i)
 
         @pl.when(m == 0)
         def _():
-            pl.semaphore_wait(barrier, jnp.where(late, cross + cores - 1 + 2 * cores, cross))
-
-        inner_copy(s, c, i, r).start()
+            pl.semaphore_wait(barrier, jnp.where(late, cross + cores - 1 + 2 * cores, chips - 1))
+
+        inner_copy(s, c, i).start()
 
         @pl.when(m == turn)
         def _():
@@ -345,22 +363,23 @@
 
     lax.fori_loop(0, early * cross * q, inner_step, 0)
     lax.fori_loop(cross, cross * nc, start_edges(in_cross), 0)
-    lax.fori_loop(early * cross, cross * nc, start_local(in_cross), 0)
+    for s in range(ranks):
+        rest_local(s).start()
     lax.fori_loop(0, cores * nc, start_edges(in_near), 0)
-    lax.fori_loop(0, cores * nc, start_local(in_near), 0)
     for copy in heat_edges():
         copy.start()
     th_local.start()
     sun_local.start()
     tables[0].start()
     tables[2].start()
-    for copy in depth_edges():
-        copy.wait()
+    settle(dext.at[pl.ds(0, 2 * EDGE)], s_recv.at[1])
 
     def outer_step(k, carry):
         s, c = in_cross(k)
-        for copy in edges(s, c):
-            copy.wait_recv()
+
+        @pl.when(s == 0)
+        def _():
+            wait_edges(c, cross * q)
 
         def sides(i, carry):
             for side in range(2):
@@ -369,21 +388,32 @@
 
         lax.fori_loop(0, q, sides, 0)
         for side in range(2):
-            outer_copy(s, c, side, r).start()
+            outer_copy(s, c, side).start()
         return carry
 
     lax.fori_loop(0, early * cross, outer_step, 0)
+
+    settle(ext.at[:, pl.ds(0, nl - early * cross * q), body], l_sem.at[early * cross])
 
     def away_step(m, carry):
         far = m < cross * nc
         k = m - cross * nc
         s = jnp.where(far, lax.rem(m, cross), cross + k // nc)
         c = jnp.where(far, m // cross, lax.rem(k, nc))
+
+        @pl.when(jnp.logical_and(far, s == 0))
+        def _():
+            wait_edges(c, cross * q)
+
+        @pl.when(jnp.logical_and(jnp.logical_not(far), c == 0))
+        def _():
+            wait_edges(nc + s - cross, per)
+
         advance(s, c, put_adv)
 
         @pl.when(m != cross * nc - 1)
         def _():
-            block_copy(s, c, r).start()
+            block_copy(s, c).start()
 
         return carry
 
@@ -393,6 +423,7 @@
         advance(ranks - 1, c, put_cells)
         return carry
 
+    wait_edges(nc + cores - 1, per)
     lax.fori_loop(0, nc, own_step, 0)
 
     above = jnp.zeros((rows, width), jnp.float32)
@@ -412,12 +443,11 @@
         def _():
             over_copy(k).start()
 
-    block_copy(cross - 1, nc - 1, r).start()
+    block_copy(cross - 1, nc - 1).start()
 
     th_local.wait()
     sun_local.wait()
-    for copy in heat_edges():
-        copy.wait()
+    settle(hext.at[:, pl.ds(0, 2 * EDGE)], s_recv.at[0])
     lane = lane_index((full, width))
     coriolis = coriolis_base + beta_plane * lane.astype(jnp.float32) / width
 
@@ -471,28 +501,8 @@
             above = above + over[k - 1]
         aux[0] = (above + clear) * scale
 
-    def wait_far(c):
-        def step(s, carry):
-            block_copy(s, c, source(s)).wait_recv()
-            return carry
-        return step
-
     def react_chunk(c, carry):
-        @pl.when(c < early)
-        def _():
-            def first_parts(s, carry):
-                for i in range(q):
-                    inner_copy(s, c, i, source(s)).wait_recv()
-                for side in range(2):
-                    outer_copy(s, c, side, source(s)).wait_recv()
-                return carry
-
-            lax.fori_loop(0, cross, first_parts, 0)
-            lax.fori_loop(cross, ranks - 1, wait_far(c), 0)
-
-        @pl.when(c >= early)
-        def _():
-            lax.fori_loop(0, ranks - 1, wait_far(c), 0)
+        wait_blocks(c)
 
         def one_level(j, carry):
             i = c * q + j
@@ -514,47 +524,24 @@
 
     lax.fori_loop(0, nc - 1, react_chunk, 0)
 
-    def drain_edges(m, carry):
-        for copy in edges(m // nc, lax.rem(m, nc)):
-            copy.wait_send()
-        return carry
-
-    lax.fori_loop(0, ranks * nc, drain_edges, 0)
+    settle(fc.at[:, :, pl.ds(0, LOW_FLOW + HIGH_FLOW)], edge_send.at[0])
+    settle(sp.at[:, :, pl.ds(0, 2 * EDGE)], edge_send.at[1])
+    settle(th.at[:, pl.ds(0, 2 * EDGE)], edge_send.at[2])
+    settle(dep.at[pl.ds(0, 2 * EDGE)], edge_send.at[3])
     for k in range(1, chips):
         @pl.when(gets_over(k))
         def _():
             over_copy(k).wait_send()
 
-    def drain_first(k, carry):
-        s, c = in_cross(k)
-        for i in range(q):
-            inner_copy(s, c, i, r).wait_send()
-        for side in range(2):
-            outer_copy(s, c, side, r).wait_send()
-        return carry
-
-    lax.fori_loop(0, early * cross, drain_first, 0)
-
-    def drain_far(m, carry):
-        s, c = in_cross(m)
-        block_copy(s, c, r).wait_send()
-        return carry
-
-    lax.fori_loop(early * cross, cross * nc, drain_far, 0)
-
-    def drain_near(m, carry):
-        block_copy(cross + m // nc, lax.rem(m, nc), r).wait_send()
-        return carry
-
-    lax.fori_loop(0, (cores - 1) * nc, drain_near, 0)
-    lax.fori_loop(0, ranks - 1, wait_far(nc - 1), 0)
+    settle(adv.at[:, pl.ds(0, (ranks - 1) * per)], d_send.at[0])
+    wait_blocks(nc - 1)
 
 
 def finish_kernel(
     levels, q,
     cells, vel, heat, aux, eaten, att, rate,
     out, vel_out, temp_out,
-    last, warm, sat, pull, eater, sem, last_sem,
+    last, warm, sat, pull, eater, sem,
 ):
     count, per = cells.shape[:2]
     r = lax.axis_index("tracer")
@@ -571,7 +558,7 @@
         eater[eaten[t]] = t
 
     def level_copy(j):
-        return pltpu.make_async_copy(last.at[j], out.at[:, done + j], last_sem.at[j])
+        return pltpu.make_async_copy(last.at[j], out.at[:, done + j], sem.at[4])
 
     def one_level(j, tau):
         def put(t, x):
@@ -591,8 +578,7 @@
     warm_copy.start()
     for copy in copies:
         copy.wait()
-    for j in range(q):
-        level_copy(j).wait()
+    pltpu.make_async_copy(last, last, sem.at[4]).wait()
     warm_copy.wait()
 
 
@@ -613,11 +599,11 @@
         nt, nl, rows, width = species_amounts.shape
         per = nl // ranks
         q = 2 if per % 2 == 0 else 1
-        chunks = nl // q
+        nc = per // q
         count = ranks * nt
         cross = ranks - cores
         chips = ranks // cores
-        early = min(2, per // q - 1)
+        early = min(2, nc - 1)
         full = rows + 2 * PAD
         f32 = jnp.float32
         any_space = pl.BlockSpec(memory_space=pl.ANY)
@@ -651,14 +637,9 @@
                 pltpu.VMEM((count, rows, width), f32),
                 pltpu.VMEM((count, rows, width), f32),
                 pltpu.SMEM((count,), jnp.int32),
-                dma((chunks, 2)), dma((chunks, 2)),
-                dma((chunks, 2)), dma((chunks, 2)),
-                dma((2, 2)), dma((2, 2)),
-                dma((chunks,)), dma((chunks,)),
-                dma((early, cross, q)), dma((early, cross, q)),
-                dma((early, cross, 2)), dma((early, cross, 2)),
-                dma((chips,)), dma((chips,)), dma((1,)), dma((1,)),
-                dma((chunks,)), dma((chunks,)), dma((3,)), dma((3,)),
+                dma((4,)), dma((nc + cores,)), dma((nc + cores,)), dma((2,)),
+                dma((1,)), dma((nc,)), dma((chips,)), dma((chips,)),
+                dma((early * cross + 1,)), dma((2,)), dma((3,)), dma((3,)),
                 pltpu.SemaphoreType.REGULAR,
             ],
             compiler_params=pltpu.CompilerParams(
@@ -687,7 +668,7 @@
                 pltpu.VMEM((count, rows, width), f32),
                 pltpu.VMEM((count, rows, width), f32),
                 pltpu.SMEM((count,), jnp.int32),
-                dma((4,)), dma((q,)),
+                dma((5,)),
             ],
             compiler_params=pltpu.CompilerParams(vmem_limit_bytes=32 << 20),
             name="finish",

time: 56.5 us -> 55.9 us (0.989); the launches traced: 55.5 us -> 55.8 us
  no operation moved by 1% of the time
where the time goes in v3:
time: 55.9 us; the launch traced here: 55.8 us
  Pallas kernels  55.1 us (99%)
  between operations  0.69 us (1%)
    pallas_call x1, Pallas kernels, on_device(): pl.pallas_call(functools.partial(transport_kernel, tiles, ranks, cores, q...  52.3 us
    pallas_call x1, Pallas kernels, on_device(): pl.pallas_call(functools.partial(finish_kernel, nl, q), out_shape=(jax.Sh...  2.72 us

profile of v3, /device:TPU:0, one launch (start us, length us, event | category | flops | bytes accessed | tf_op | source)
XLA Modules:
  0.0 55.8 jit_solution(2789783952014032512)
XLA Ops:
  0.6 0.0 copy-start.2
  0.6 0.0 copy-start.1
  0.7 0.0 copy-start
  0.7 52.3 %transport.1 = (f32[32,8,32,128]{3,2,1,0:T(8,128)S(1)}, f32[2,8,32,128]{3,2,1,0:T(8,128)S(1)}, f32[8,32,128]{2,1,0:T(8,128)S(1)}, f32[3,32,128]{2,1,0:T(8,128)S(1)}) custom-call(f32[8,32,32,128]{3,2,1,0:T(8,128)} %sp.1, f32[2,32,32,128]{3,2,1,0:T(8,128)} %fc.1, f32[8,32,128]{2,1,0:T(8,128)} %th.1, s32[32,128]{1,0:T(8,128)} %dep.1, f32[32,128]{1,0:T(8,128)} %sun.1, ...), custom_call_target="tpu_custom_call" | custom-call | tf_op jit(solution)/shard_map/transport/pallas_call | solution.py:613
  53.0 0.0 copy-done.2
  53.0 0.0 copy-done.1
  53.0 0.0 copy-done
  53.0 2.7 %finish.1 = (f32[32,8,32,128]{3,2,1,0:T(8,128)}, f32[2,8,32,128]{3,2,1,0:T(8,128)}, f32[8,32,128]{2,1,0:T(8,128)}) custom-call(f32[32,8,32,128]{3,2,1,0:T(8,128)S(1)} %get-tuple-element.7.cells, f32[2,8,32,128]{3,2,1,0:T(8,128)S(1)} %get-tuple-element.8.vel, f32[8,32,128]{2,1,0:T(8,128)S(1)} %get-tuple-element.9.heat, ...), custom_call_target="tpu_custom_call" | custom-call | tf_op jit(solution)/shard_map/finish/pallas_call | solution.py:656
Async XLA Ops:
  0.6 52.4 %copy-start.2 = (f32[32]{0:T(128)S(1)}, f32[32]{0:T(128)}, u32[]{:S(2)}) copy-start(f32[32]{0:T(128)} %rate.1) | copy-start | bytes 388
  0.6 52.4 %copy-start.1 = (f32[32]{0:T(128)S(1)}, f32[32]{0:T(128)}, u32[]{:S(2)}) copy-start(f32[32]{0:T(128)} %att.1) | copy-start | bytes 388
  0.7 52.4 %copy-start = (s32[32]{0:T(128)S(1)}, s32[32]{0:T(128)}, u32[]{:S(2)}) copy-start(s32[32]{0:T(128)} %eaten.1) | copy-start | bytes 388

commit v4 on v3

--- a/solution.py
+++ b/solution.py
@@ -51,7 +51,7 @@
 
 
 def minmod(a, b):
-    return jnp.maximum(jnp.minimum(a, b), 0.0) + jnp.minimum(jnp.maximum(a, b), 0.0)
+    return jnp.maximum(jnp.minimum(a, b), jnp.minimum(jnp.maximum(a, b), 0.0))
 
 
 def laplacian(x):
@@ -60,12 +60,13 @@
 
 def substep(c, es, ns, lane):
     last = c.shape[1] - 1
-    d = east(c) - c
-    half = 0.5 * minmod(west(d), d)
+    e = 0.5 * c
+    d = east(e) - e
+    half = minmod(west(d), d)
     flux = es * jnp.where(es > 0.0, c + half, east(c - half))
     spread = flux - west(flux)
-    d = jnp.where(lane == last, 0.0, pltpu.roll(c, last, 1)) - c
-    half = 0.5 * minmod(jnp.where(lane == 0, c, pltpu.roll(d, 1, 1)), d)
+    d = jnp.where(lane == last, 0.0, pltpu.roll(e, last, 1)) - e
+    half = minmod(jnp.where(lane == 0, e, pltpu.roll(d, 1, 1)), d)
     flux = ns * jnp.where(ns > 0.0, c + half, pltpu.roll(c - half, last, 1))
     return c - (spread + (flux - pltpu.roll(flux, 1, 1)))
 
@@ -103,7 +104,7 @@
     count = ranks * nt
     chips = ranks // cores
     cross = ranks - cores
-    full = rows + 2 * PAD
+    full = rows + PAD
     r = lax.axis_index("tracer")
     z = lax.axis_index("tile")
     a, b = r // cores, lax.rem(r, cores)
@@ -136,7 +137,7 @@
             ),
             pltpu.make_async_remote_copy(
                 src.at[lead + (pl.ds(0, high),)],
-                dst.at[lead + (pl.ds(PAD + rows, high),)],
+                dst.at[lead + (pl.ds(0, high),)],
                 send, recv, device_id={"tile": down}, device_id_type=MESH,
             ),
         )
@@ -283,6 +284,11 @@
 
         tot[block, kept] = lax.fori_loop(0, nt, one_tracer, tot[block, kept], unroll=True)
 
+    def strip(ref, *lead):
+        return jnp.concatenate(
+            [ref[lead + (pl.ds(full - TILE, TILE),)], ref[lead + (pl.ds(0, PAD + TILE),)]], axis=0
+        )
+
     def put_adv(t, lev, kept, c):
         adv[t, lev, kept] = c
 
@@ -293,11 +299,27 @@
         lev = first_level(s, c) + i
         advect(lev, target(s), PAD, rows, EDGE, EDGE, rows - 2 * EDGE, put_adv)
 
-    def advance_outer(s, c, i, side):
+    def advance_outer(s, c, i):
         lev = first_level(s, c) + i
-        base = side * (rows - PAD)
-        skip, first = (TILE + EDGE, rows - EDGE) if side else (PAD, 0)
-        advect(lev, target(s), base, TILE + 2 * PAD, skip, first, EDGE, put_adv)
+        block = target(s)
+        size = TILE + PAD + TILE
+        lane = lane_index((size, width))
+        wet = jnp.where(lev < strip(dext), 1.0, 0.0)
+        es = sub_step * (strip(fext, 0, lev) * wet * east(wet))
+        ns = sub_step * (strip(fext, 1, lev) * wet * north(wet))
+        high, low = slice(TILE - EDGE, TILE), slice(TILE + PAD, TILE + PAD + EDGE)
+        high_rows, low_rows = pl.ds(rows - EDGE, EDGE), pl.ds(0, EDGE)
+
+        def one_tracer(t, acc):
+            c = substep(strip(ext, t, lev), es, ns, lane)
+            c = substep(c, es, ns, lane)
+            adv[t, lev, high_rows] = c[high]
+            adv[t, lev, low_rows] = c[low]
+            return acc + att[r * nt + t] * jnp.abs(c)
+
+        acc = lax.fori_loop(0, nt, one_tracer, jnp.zeros((size, width), jnp.float32), unroll=True)
+        tot[block, high_rows] += acc[high]
+        tot[block, low_rows] += acc[low]
 
     def advance(s, c, put):
         block = target(s)
@@ -382,8 +404,7 @@
             wait_edges(c, cross * q)
 
         def sides(i, carry):
-            for side in range(2):
-                advance_outer(s, c, i, side)
+            advance_outer(s, c, i)
             return carry
 
         lax.fori_loop(0, q, sides, 0)
@@ -604,7 +625,7 @@
         cross = ranks - cores
         chips = ranks // cores
         early = min(2, nc - 1)
-        full = rows + 2 * PAD
+        full = rows + PAD
         f32 = jnp.float32
         any_space = pl.BlockSpec(memory_space=pl.ANY)
         vmem = pl.BlockSpec(memory_space=pltpu.VMEM)

time: 55.9 us -> 55.3 us (0.989)
  Pallas kernels: 55.1 us -> 54.5 us
    pallas_call x1, Pallas kernels: 52.3 us -> 51.8 us  [on_device(): pl.pallas_call(functools.partial(transport_kernel, tiles, ranks, cores, q...]
where the time goes in v4:
time: 55.3 us; the launch traced here: 55.2 us
  Pallas kernels  54.5 us (99%)
  between operations  0.69 us (1%)
    pallas_call x1, Pallas kernels, on_device(): pl.pallas_call(functools.partial(transport_kernel, tiles, ranks, cores, q...  51.8 us
    pallas_call x1, Pallas kernels, on_device(): pl.pallas_call(functools.partial(finish_kernel, nl, q), out_shape=(jax.Sh...  2.72 us

profile of v4, /device:TPU:0, one launch (start us, length us, event | category | flops | bytes accessed | tf_op | source)
XLA Modules:
  0.0 55.2 jit_solution(13556307038518863181)
XLA Ops:
  0.6 0.0 copy-start.2
  0.6 0.0 copy-start.1
  0.7 0.0 copy-start
  0.7 51.8 %transport.1 = (f32[32,8,32,128]{3,2,1,0:T(8,128)S(1)}, f32[2,8,32,128]{3,2,1,0:T(8,128)S(1)}, f32[8,32,128]{2,1,0:T(8,128)S(1)}, f32[3,32,128]{2,1,0:T(8,128)S(1)}) custom-call(f32[8,32,32,128]{3,2,1,0:T(8,128)} %sp.1, f32[2,32,32,128]{3,2,1,0:T(8,128)} %fc.1, f32[8,32,128]{2,1,0:T(8,128)} %th.1, s32[32,128]{1,0:T(8,128)} %dep.1, f32[32,128]{1,0:T(8,128)} %sun.1, ...), custom_call_target="tpu_custom_call" | custom-call | tf_op jit(solution)/shard_map/transport/pallas_call | solution.py:634
  52.4 0.0 copy-done.2
  52.4 0.0 copy-done.1
  52.5 0.0 copy-done
  52.5 2.7 %finish.1 = (f32[32,8,32,128]{3,2,1,0:T(8,128)}, f32[2,8,32,128]{3,2,1,0:T(8,128)}, f32[8,32,128]{2,1,0:T(8,128)}) custom-call(f32[32,8,32,128]{3,2,1,0:T(8,128)S(1)} %get-tuple-element.7.cells, f32[2,8,32,128]{3,2,1,0:T(8,128)S(1)} %get-tuple-element.8.vel, f32[8,32,128]{2,1,0:T(8,128)S(1)} %get-tuple-element.9.heat, ...), custom_call_target="tpu_custom_call" | custom-call | tf_op jit(solution)/shard_map/finish/pallas_call | solution.py:677
Async XLA Ops:
  0.6 51.8 %copy-start.2 = (f32[32]{0:T(128)S(1)}, f32[32]{0:T(128)}, u32[]{:S(2)}) copy-start(f32[32]{0:T(128)} %rate.1) | copy-start | bytes 388
  0.6 51.8 %copy-start.1 = (f32[32]{0:T(128)S(1)}, f32[32]{0:T(128)}, u32[]{:S(2)}) copy-start(f32[32]{0:T(128)} %att.1) | copy-start | bytes 388
  0.7 51.8 %copy-start = (s32[32]{0:T(128)S(1)}, s32[32]{0:T(128)}, u32[]{:S(2)}) copy-start(s32[32]{0:T(128)} %eaten.1) | copy-start | bytes 388

commit v5 on v4

--- a/solution.py
+++ b/solution.py
@@ -105,18 +105,18 @@
     chips = ranks // cores
     cross = ranks - cores
     full = rows + PAD
+    parts = 2 if nt % 2 == 0 else 1
+    some = nt // parts
     r = lax.axis_index("tracer")
     z = lax.axis_index("tile")
     a, b = r // cores, lax.rem(r, cores)
     up, down = lax.rem(z + 1, tiles), lax.rem(z + tiles - 1, tiles)
 
-    def steps(s):
+    def target(s):
         k = lax.rem(s, cores)
-        return lax.rem(1 + s // cores, chips), jnp.where(s < cross, k, cores - 1 - k)
-
-    def target(s):
-        ka, kb = steps(s)
-        return lax.rem(a + ka, chips) * cores + lax.rem(b + kb, cores)
+        chip = lax.rem(a + 1 + s // cores, chips)
+        core = jnp.where(s < cross, k, lax.rem(b + cores - 1 - k, cores))
+        return chip * cores + core
 
     def first_level(s, c):
         return target(s) * per + c * q
@@ -182,10 +182,10 @@
             device_id={"tracer": target(s)}, device_id_type=MESH,
         )
 
-    def inner_copy(s, c, i):
+    def inner_copy(s, c, i, h):
         return pltpu.make_async_remote_copy(
-            adv.at[:, first_level(s, c) + i, inner],
-            cells.at[mine, c * q + i, inner],
+            adv.at[pl.ds(h * some, some), first_level(s, c) + i, inner],
+            cells.at[pl.ds(r * nt + h * some, some), c * q + i, inner],
             d_send.at[0], d_recv.at[c],
             device_id={"tracer": target(s)}, device_id_type=MESH,
         )
@@ -229,12 +229,12 @@
     last_core = a * cores + cores - 1
     late = b == cores - 1
     barrier = pltpu.get_barrier_semaphore()
-    for s in range(0, cross, cores):
+    for s in range(cores - 1, cross, cores):
         pl.semaphore_signal(barrier, inc=1, device_id={"tracer": target(s)}, device_id_type=MESH)
     if cores > 1:
         @pl.when(jnp.logical_not(late))
         def _():
-            for s in range(1, cross, cores):
+            for s in range(0, cross, cores):
                 pl.semaphore_signal(
                     barrier, inc=1, device_id={"tracer": target(s)}, device_id_type=MESH
                 )
@@ -268,7 +268,7 @@
     dep_local.wait()
     tables[1].wait()
 
-    def advect(lev, block, base, size, skip, first, keep, put):
+    def advect(lev, block, base, size, skip, first, keep, put, t_0=0, some=nt):
         window = pl.ds(base, size)
         kept = pl.ds(first, keep)
         lane = lane_index((size, width))
@@ -276,13 +276,14 @@
         es = sub_step * (fext[0, lev, window] * wet * east(wet))
         ns = sub_step * (fext[1, lev, window] * wet * north(wet))
 
-        def one_tracer(t, acc):
+        def one_tracer(k, acc):
+            t = t_0 + k
             c = substep(ext[t, lev, window], es, ns, lane)
             c = substep(c, es, ns, lane)[skip:skip + keep]
             put(t, lev, kept, c)
             return acc + att[r * nt + t] * jnp.abs(c)
 
-        tot[block, kept] = lax.fori_loop(0, nt, one_tracer, tot[block, kept], unroll=True)
+        tot[block, kept] = lax.fori_loop(0, some, one_tracer, tot[block, kept], unroll=True)
 
     def strip(ref, *lead):
         return jnp.concatenate(
@@ -295,9 +296,9 @@
     def put_cells(t, lev, kept, c):
         cells[r * nt + t, lev - r * per, kept] = c
 
-    def advance_inner(s, c, i):
+    def advance_inner(s, c, i, h):
         lev = first_level(s, c) + i
-        advect(lev, target(s), PAD, rows, EDGE, EDGE, rows - 2 * EDGE, put_adv)
+        advect(lev, target(s), PAD, rows, EDGE, EDGE, rows - 2 * EDGE, put_adv, h * some, some)
 
     def advance_outer(s, c, i):
         lev = first_level(s, c) + i
@@ -338,31 +339,32 @@
             return carry
         return step
 
-    turn = jnp.where(late, 0, early * q - 1)
+    turn = jnp.where(late, 0, early * q * parts - 1)
 
     def inner_step(m, carry):
-        k, i = m // q, lax.rem(m, q)
+        h = lax.rem(m, parts)
+        k, i = m // (q * parts), lax.rem(m // parts, q)
         s, c = k // early, lax.rem(k, early)
 
         @pl.when(m == 0)
         def _():
             flow_local(0).wait()
 
-        @pl.when(m == early * q)
+        @pl.when(m == early * q * parts)
         def _():
             settle(fext.at[:, pl.ds(0, (ranks - 1) * per), body], lf_sem.at[1])
 
-        @pl.when(i == 0)
+        @pl.when(jnp.logical_and(i == 0, h == 0))
         def _():
             early_local(k).wait()
 
-        advance_inner(s, c, i)
+        advance_inner(s, c, i, h)
 
         @pl.when(m == 0)
         def _():
             pl.semaphore_wait(barrier, jnp.where(late, cross + cores - 1 + 2 * cores, chips - 1))
 
-        inner_copy(s, c, i).start()
+        inner_copy(s, c, i, h).start()
 
         @pl.when(m == turn)
         def _():
@@ -383,7 +385,7 @@
 
         return carry
 
-    lax.fori_loop(0, early * cross * q, inner_step, 0)
+    lax.fori_loop(0, early * cross * q * parts, inner_step, 0)
     lax.fori_loop(cross, cross * nc, start_edges(in_cross), 0)
     for s in range(ranks):
         rest_local(s).start()
@@ -560,9 +562,9 @@
 
 def finish_kernel(
     levels, q,
-    cells, vel, heat, aux, eaten, att, rate,
+    cells, vel, heat, aux, eaten_in, att_in, rate_in,
     out, vel_out, temp_out,
-    last, warm, sat, pull, eater, sem,
+    eaten, att, rate, last, warm, sat, pull, eater, sem, t_sem,
 ):
     count, per = cells.shape[:2]
     r = lax.axis_index("tracer")
@@ -573,8 +575,14 @@
         pltpu.make_async_copy(vel, vel_out, sem.at[1]),
         pltpu.make_async_copy(heat.at[pl.ds(0, done)], temp_out.at[pl.ds(0, done)], sem.at[2]),
     ]
-    for copy in copies:
+    tables = [
+        pltpu.make_async_copy(src, dst, t_sem.at[k])
+        for k, (src, dst) in enumerate(((eaten_in, eaten), (att_in, att), (rate_in, rate)))
+    ]
+    for copy in tables + copies:
         copy.start()
+    for copy in tables:
+        copy.wait()
     for t in range(count):
         eater[eaten[t]] = t
 
@@ -629,7 +637,6 @@
         f32 = jnp.float32
         any_space = pl.BlockSpec(memory_space=pl.ANY)
         vmem = pl.BlockSpec(memory_space=pltpu.VMEM)
-        smem = pl.BlockSpec(memory_space=pltpu.SMEM)
         dma = pltpu.SemaphoreType.DMA
         cells, vel, heat, aux = pl.pallas_call(
             functools.partial(transport_kernel, tiles, ranks, cores, q, early),
@@ -681,15 +688,18 @@
                 jax.ShapeDtypeStruct((2, per, rows, width), f32),
                 jax.ShapeDtypeStruct((per, rows, width), f32),
             ),
-            in_specs=[vmem] * 4 + [smem] * 3,
+            in_specs=[vmem] * 4 + [any_space] * 3,
             out_specs=(any_space, any_space, any_space),
             scratch_shapes=[
+                pltpu.SMEM((count,), jnp.int32),
+                pltpu.SMEM((count,), f32),
+                pltpu.SMEM((count,), f32),
                 pltpu.VMEM((q, count, rows, width), f32),
                 pltpu.VMEM((q, rows, width), f32),
                 pltpu.VMEM((count, rows, width), f32),
                 pltpu.VMEM((count, rows, width), f32),
                 pltpu.SMEM((count,), jnp.int32),
-                dma((5,)),
+                dma((5,)), dma((3,)),
             ],
             compiler_params=pltpu.CompilerParams(vmem_limit_bytes=32 << 20),
             name="finish",

time: 55.3 us -> 57.8 us (1.045)
  the two profiles are of different devices: /device:TPU:0 before, /device:TPU:1 now
where the time goes in v5:
time: 57.8 us; the launch traced here: 57.7 us
  Pallas kernels  57 us (99%)
  between operations  0.69 us (1%)
    pallas_call x1, Pallas kernels, on_device(): pl.pallas_call(functools.partial(transport_kernel, tiles, ranks, cores, q...  54.8 us
    pallas_call x1, Pallas kernels, on_device(): pl.pallas_call(functools.partial(finish_kernel, nl, q), out_shape=(jax.Sh...  2.2 us

profile of v5, /device:TPU:1, one launch (start us, length us, event | category | flops | bytes accessed | tf_op | source)
XLA Modules:
  0.0 57.7 jit_solution(14937821696496768760)
XLA Ops:
  0.6 0.0 copy-start.2
  0.6 0.0 copy-start.1
  0.7 0.0 copy-start
  0.7 54.8 %transport.1 = (f32[32,8,32,128]{3,2,1,0:T(8,128)S(1)}, f32[2,8,32,128]{3,2,1,0:T(8,128)S(1)}, f32[8,32,128]{2,1,0:T(8,128)S(1)}, f32[3,32,128]{2,1,0:T(8,128)S(1)}) custom-call(f32[8,32,32,128]{3,2,1,0:T(8,128)} %sp.1, f32[2,32,32,128]{3,2,1,0:T(8,128)} %fc.1, f32[8,32,128]{2,1,0:T(8,128)} %th.1, s32[32,128]{1,0:T(8,128)} %dep.1, f32[32,128]{1,0:T(8,128)} %sun.1, ...), custom_call_target="tpu_custom_call" | custom-call | tf_op jit(solution)/shard_map/transport/pallas_call | solution.py:641
  55.4 0.0 copy-done.2
  55.4 0.0 copy-done.1
  55.5 0.0 copy-done
  55.5 2.2 %finish.1 = (f32[32,8,32,128]{3,2,1,0:T(8,128)}, f32[2,8,32,128]{3,2,1,0:T(8,128)}, f32[8,32,128]{2,1,0:T(8,128)}) custom-call(f32[32,8,32,128]{3,2,1,0:T(8,128)S(1)} %get-tuple-element.7.cells, f32[2,8,32,128]{3,2,1,0:T(8,128)S(1)} %get-tuple-element.8.vel, f32[8,32,128]{2,1,0:T(8,128)S(1)} %get-tuple-element.9.heat, ...), custom_call_target="tpu_custom_call" | custom-call | tf_op jit(solution)/shard_map/finish/pallas_call | solution.py:684
Async XLA Ops:
  0.6 54.8 %copy-start.2 = (f32[32]{0:T(128)S(1)}, f32[32]{0:T(128)}, u32[]{:S(2)}) copy-start(f32[32]{0:T(128)} %rate_in.3) | copy-start | bytes 388
  0.6 54.8 %copy-start.1 = (f32[32]{0:T(128)S(1)}, f32[32]{0:T(128)}, u32[]{:S(2)}) copy-start(f32[32]{0:T(128)} %att_in.3) | copy-start | bytes 388
  0.7 54.8 %copy-start = (s32[32]{0:T(128)S(1)}, s32[32]{0:T(128)}, u32[]{:S(2)}) copy-start(s32[32]{0:T(128)} %eaten_in.3) | copy-start | bytes 388

commit v6 on v4

--- a/solution.py
+++ b/solution.py
@@ -110,13 +110,11 @@
     a, b = r // cores, lax.rem(r, cores)
     up, down = lax.rem(z + 1, tiles), lax.rem(z + tiles - 1, tiles)
 
-    def steps(s):
+    def target(s):
         k = lax.rem(s, cores)
-        return lax.rem(1 + s // cores, chips), jnp.where(s < cross, k, cores - 1 - k)
-
-    def target(s):
-        ka, kb = steps(s)
-        return lax.rem(a + ka, chips) * cores + lax.rem(b + kb, cores)
+        chip = lax.rem(a + 1 + s // cores, chips)
+        core = jnp.where(s < cross, k, lax.rem(b + cores - 1 - k, cores))
+        return chip * cores + core
 
     def first_level(s, c):
         return target(s) * per + c * q
@@ -229,12 +227,12 @@
     last_core = a * cores + cores - 1
     late = b == cores - 1
     barrier = pltpu.get_barrier_semaphore()
-    for s in range(0, cross, cores):
+    for s in range(cores - 1, cross, cores):
         pl.semaphore_signal(barrier, inc=1, device_id={"tracer": target(s)}, device_id_type=MESH)
     if cores > 1:
         @pl.when(jnp.logical_not(late))
         def _():
-            for s in range(1, cross, cores):
+            for s in range(0, cross, cores):
                 pl.semaphore_signal(
                     barrier, inc=1, device_id={"tracer": target(s)}, device_id_type=MESH
                 )
@@ -560,9 +558,9 @@
 
 def finish_kernel(
     levels, q,
-    cells, vel, heat, aux, eaten, att, rate,
+    cells, vel, heat, aux, eaten_in, att_in, rate_in,
     out, vel_out, temp_out,
-    last, warm, sat, pull, eater, sem,
+    eaten, att, rate, last, warm, sat, pull, eater, sem, t_sem,
 ):
     count, per = cells.shape[:2]
     r = lax.axis_index("tracer")
@@ -573,8 +571,14 @@
         pltpu.make_async_copy(vel, vel_out, sem.at[1]),
         pltpu.make_async_copy(heat.at[pl.ds(0, done)], temp_out.at[pl.ds(0, done)], sem.at[2]),
     ]
-    for copy in copies:
+    tables = [
+        pltpu.make_async_copy(src, dst, t_sem.at[k])
+        for k, (src, dst) in enumerate(((eaten_in, eaten), (att_in, att), (rate_in, rate)))
+    ]
+    for copy in tables + copies:
         copy.start()
+    for copy in tables:
+        copy.wait()
     for t in range(count):
         eater[eaten[t]] = t
 
@@ -629,7 +633,6 @@
         f32 = jnp.float32
         any_space = pl.BlockSpec(memory_space=pl.ANY)
         vmem = pl.BlockSpec(memory_space=pltpu.VMEM)
-        smem = pl.BlockSpec(memory_space=pltpu.SMEM)
         dma = pltpu.SemaphoreType.DMA
         cells, vel, heat, aux = pl.pallas_call(
             functools.partial(transport_kernel, tiles, ranks, cores, q, early),
@@ -681,15 +684,18 @@
                 jax.ShapeDtypeStruct((2, per, rows, width), f32),
                 jax.ShapeDtypeStruct((per, rows, width), f32),
             ),
-            in_specs=[vmem] * 4 + [smem] * 3,
+            in_specs=[vmem] * 4 + [any_space] * 3,
             out_specs=(any_space, any_space, any_space),
             scratch_shapes=[
+                pltpu.SMEM((count,), jnp.int32),
+                pltpu.SMEM((count,), f32),
+                pltpu.SMEM((count,), f32),
                 pltpu.VMEM((q, count, rows, width), f32),
                 pltpu.VMEM((q, rows, width), f32),
                 pltpu.VMEM((count, rows, width), f32),
                 pltpu.VMEM((count, rows, width), f32),
                 pltpu.SMEM((count,), jnp.int32),
-                dma((5,)),
+                dma((5,)), dma((3,)),
             ],
             compiler_params=pltpu.CompilerParams(vmem_limit_bytes=32 << 20),
             name="finish",

time: 55.3 us -> 54.1 us (0.978)
  the two profiles are of different devices: /device:TPU:0 before, /device:TPU:1 now
where the time goes in v6:
time: 54.1 us; the launch traced here: 54 us
  Pallas kernels  53.3 us (99%)
  between operations  0.69 us (1%)
    pallas_call x1, Pallas kernels, on_device(): pl.pallas_call(functools.partial(transport_kernel, tiles, ranks, cores, q...  51.1 us
    pallas_call x1, Pallas kernels, on_device(): pl.pallas_call(functools.partial(finish_kernel, nl, q), out_shape=(jax.Sh...  2.2 us

profile of v6, /device:TPU:1, one launch (start us, length us, event | category | flops | bytes accessed | tf_op | source)
XLA Modules:
  0.0 54.0 jit_solution(17377635980567845916)
XLA Ops:
  0.6 0.0 copy-start.2
  0.6 0.0 copy-start.1
  0.7 0.0 copy-start
  0.7 51.1 %transport.1 = (f32[32,8,32,128]{3,2,1,0:T(8,128)S(1)}, f32[2,8,32,128]{3,2,1,0:T(8,128)S(1)}, f32[8,32,128]{2,1,0:T(8,128)S(1)}, f32[3,32,128]{2,1,0:T(8,128)S(1)}) custom-call(f32[8,32,32,128]{3,2,1,0:T(8,128)} %sp.1, f32[2,32,32,128]{3,2,1,0:T(8,128)} %fc.1, f32[8,32,128]{2,1,0:T(8,128)} %th.1, s32[32,128]{1,0:T(8,128)} %dep.1, f32[32,128]{1,0:T(8,128)} %sun.1, ...), custom_call_target="tpu_custom_call" | custom-call | tf_op jit(solution)/shard_map/transport/pallas_call | solution.py:637
  51.8 0.0 copy-done.2
  51.8 0.0 copy-done.1
  51.8 0.0 copy-done
  51.8 2.2 %finish.1 = (f32[32,8,32,128]{3,2,1,0:T(8,128)}, f32[2,8,32,128]{3,2,1,0:T(8,128)}, f32[8,32,128]{2,1,0:T(8,128)}) custom-call(f32[32,8,32,128]{3,2,1,0:T(8,128)S(1)} %get-tuple-element.7.cells, f32[2,8,32,128]{3,2,1,0:T(8,128)S(1)} %get-tuple-element.8.vel, f32[8,32,128]{2,1,0:T(8,128)S(1)} %get-tuple-element.9.heat, ...), custom_call_target="tpu_custom_call" | custom-call | tf_op jit(solution)/shard_map/finish/pallas_call | solution.py:680
Async XLA Ops:
  0.6 51.1 %copy-start.2 = (f32[32]{0:T(128)S(1)}, f32[32]{0:T(128)}, u32[]{:S(2)}) copy-start(f32[32]{0:T(128)} %rate_in.3) | copy-start | bytes 388
  0.6 51.1 %copy-start.1 = (f32[32]{0:T(128)S(1)}, f32[32]{0:T(128)}, u32[]{:S(2)}) copy-start(f32[32]{0:T(128)} %att_in.3) | copy-start | bytes 388
  0.7 51.1 %copy-start = (s32[32]{0:T(128)S(1)}, s32[32]{0:T(128)}, u32[]{:S(2)}) copy-start(s32[32]{0:T(128)} %eaten_in.3) | copy-start | bytes 388

commit v7 on v6

--- a/solution.py
+++ b/solution.py
@@ -26,6 +26,7 @@
 EDGE = 4
 TILE = 8
 LOW_FLOW, HIGH_FLOW = 3, 2
+DEEP = 3
 
 HBM = pltpu.HBM
 
@@ -91,12 +92,12 @@
 
 
 def transport_kernel(
-    tiles, ranks, cores, q, early,
+    tiles, ranks, cores, q, deep,
     sp, fc, th, dep, sun, eaten_in, att_in, rate_in,
     cells, vel, heat, aux,
-    eaten, att, rate, ext, fext, hext, dext, adv, tot, pre, part, joined, over, sat, pull, eater,
+    eaten, att, rate, ext, fext, hext, dext, adv, tot, pre, part, joined, over, sat, pull, eater, raw,
     edge_send, h_recv, f_recv, s_recv, d_send, d_recv, o_send, o_recv,
-    l_sem, lf_sem, ls_sem, t_sem, ready,
+    l_sem, lf_sem, ls_sem, t_sem, r_send, r_recv, ready,
 ):
     nt, nl, rows, width = sp.shape
     per = nl // ranks
@@ -105,6 +106,7 @@
     chips = ranks // cores
     cross = ranks - cores
     full = rows + PAD
+    early = deep + cross - 1
     r = lax.axis_index("tracer")
     z = lax.axis_index("tile")
     a, b = r // cores, lax.rem(r, cores)
@@ -141,7 +143,7 @@
         )
 
     def edges(s, c):
-        g = jnp.where(s < cross, c, nc + s - cross)
+        g = jnp.where(s < cross, c, nc + (s - cross) * nc + c)
         lead = (slice(None), pl.ds(first_level(s, c), q))
         return (
             pair(fc, fext, lead, edge_send.at[0], f_recv.at[g], LOW_FLOW, HIGH_FLOW)
@@ -163,14 +165,20 @@
         sem = lf_sem.at[0] if s == 0 else lf_sem.at[1]
         return pltpu.make_async_copy(fc.at[:, lev], fext.at[:, lev, body], sem)
 
+    def early_chunk(k):
+        return jnp.where(k < deep, 0, k - deep + 1), jnp.where(k < deep, k, 0)
+
+    def edge_chunk(k):
+        return jnp.where(k < cross, k, 0), jnp.where(k < cross, 0, k - cross + 1)
+
     def early_local(k):
-        lev = pl.ds(first_level(k // early, lax.rem(k, early)), q)
+        lev = pl.ds(first_level(*early_chunk(k)), q)
         return pltpu.make_async_copy(sp.at[:, lev], ext.at[:, lev, body], l_sem.at[k])
 
     def rest_local(s):
-        skip = early if s < cross else 0
+        skip = deep if s == 0 else 1 if s < cross else 0
         lev = pl.ds(first_level(s, skip), per - skip * q)
-        return pltpu.make_async_copy(sp.at[:, lev], ext.at[:, lev, body], l_sem.at[early * cross])
+        return pltpu.make_async_copy(sp.at[:, lev], ext.at[:, lev, body], l_sem.at[early])
 
     def block_copy(s, c):
         return pltpu.make_async_remote_copy(
@@ -184,7 +192,7 @@
         return pltpu.make_async_remote_copy(
             adv.at[:, first_level(s, c) + i, inner],
             cells.at[mine, c * q + i, inner],
-            d_send.at[0], d_recv.at[c],
+            d_send.at[1], d_recv.at[jnp.where(c == 0, nc, c)],
             device_id={"tracer": target(s)}, device_id_type=MESH,
         )
 
@@ -193,9 +201,22 @@
         return pltpu.make_async_remote_copy(
             adv.at[:, pl.ds(first_level(s, c), q), edge],
             cells.at[mine, pl.ds(c * q, q), edge],
-            d_send.at[0], d_recv.at[c],
+            d_send.at[2], d_recv.at[c],
             device_id={"tracer": target(s)}, device_id_type=MESH,
         )
+
+    def raw_copy():
+        return pltpu.make_async_remote_copy(
+            sp.at[:, first_level(0, 0)], raw, r_send.at[0], r_recv.at[0],
+            device_id={"tracer": target(0)}, device_id_type=MESH,
+        )
+
+    def wait_first():
+        settle(ext.at[:, pl.ds(0, q * (cross + rows // TILE)), pl.ds(0, TILE)], d_recv.at[0])
+        for pieces, mask in ((cross * q, late), (cross * q - 1, jnp.logical_not(late))):
+            @pl.when(mask)
+            def _():
+                settle(ext.at[:, pl.ds(0, pieces), inner], d_recv.at[nc])
 
     def wait_blocks(c):
         settle(cells.at[pl.ds(0, (ranks - 1) * nt), pl.ds(c * q, q)], d_recv.at[c])
@@ -258,15 +279,20 @@
         early_local(k).start()
         return carry
 
-    lax.fori_loop(0, early * cross, start_early, 0)
+    lax.fori_loop(0, early, start_early, 0)
     for s in range(1, ranks):
         flow_local(s).start()
+
+    @pl.when(jnp.logical_not(late))
+    def _():
+        pl.semaphore_wait(barrier, chips - 1)
+        raw_copy().start()
 
     tot[...] = jnp.zeros_like(tot)
     dep_local.wait()
     tables[1].wait()
 
-    def advect(lev, block, base, size, skip, first, keep, put):
+    def advect(lev, block, base, size, skip, first, keep, put, take=None, owner=r):
         window = pl.ds(base, size)
         kept = pl.ds(first, keep)
         lane = lane_index((size, width))
@@ -275,10 +301,10 @@
         ns = sub_step * (fext[1, lev, window] * wet * north(wet))
 
         def one_tracer(t, acc):
-            c = substep(ext[t, lev, window], es, ns, lane)
+            c = substep(take(t) if take else ext[t, lev, window], es, ns, lane)
             c = substep(c, es, ns, lane)[skip:skip + keep]
             put(t, lev, kept, c)
-            return acc + att[r * nt + t] * jnp.abs(c)
+            return acc + att[owner * nt + t] * jnp.abs(c)
 
         tot[block, kept] = lax.fori_loop(0, nt, one_tracer, tot[block, kept], unroll=True)
 
@@ -336,17 +362,17 @@
             return carry
         return step
 
-    turn = jnp.where(late, 0, early * q - 1)
+    turn = jnp.where(late, 0, deep * q - 1)
 
     def inner_step(m, carry):
         k, i = m // q, lax.rem(m, q)
-        s, c = k // early, lax.rem(k, early)
+        s, c = early_chunk(k)
 
         @pl.when(m == 0)
         def _():
             flow_local(0).wait()
 
-        @pl.when(m == early * q)
+        @pl.when(m == deep * q)
         def _():
             settle(fext.at[:, pl.ds(0, (ranks - 1) * per), body], lf_sem.at[1])
 
@@ -354,13 +380,15 @@
         def _():
             early_local(k).wait()
 
-        advance_inner(s, c, i)
-
-        @pl.when(m == 0)
-        def _():
-            pl.semaphore_wait(barrier, jnp.where(late, cross + cores - 1 + 2 * cores, chips - 1))
-
-        inner_copy(s, c, i).start()
+        @pl.when(jnp.logical_or(late, m > 0))
+        def _():
+            advance_inner(s, c, i)
+
+            @pl.when(m == 0)
+            def _():
+                pl.semaphore_wait(barrier, cross + cores - 1 + 2 * cores)
+
+            inner_copy(s, c, i).start()
 
         @pl.when(m == turn)
         def _():
@@ -381,7 +409,7 @@
 
         return carry
 
-    lax.fori_loop(0, early * cross * q, inner_step, 0)
+    lax.fori_loop(0, early * q, inner_step, 0)
     lax.fori_loop(cross, cross * nc, start_edges(in_cross), 0)
     for s in range(ranks):
         rest_local(s).start()
@@ -395,7 +423,7 @@
     settle(dext.at[pl.ds(0, 2 * EDGE)], s_recv.at[1])
 
     def outer_step(k, carry):
-        s, c = in_cross(k)
+        s, c = edge_chunk(k)
 
         @pl.when(s == 0)
         def _():
@@ -410,9 +438,9 @@
             outer_copy(s, c, side).start()
         return carry
 
-    lax.fori_loop(0, early * cross, outer_step, 0)
-
-    settle(ext.at[:, pl.ds(0, nl - early * cross * q), body], l_sem.at[early * cross])
+    lax.fori_loop(0, early, outer_step, 0)
+
+    settle(ext.at[:, pl.ds(0, nl - early * q), body], l_sem.at[early])
 
     def away_step(m, carry):
         far = m < cross * nc
@@ -420,29 +448,44 @@
         s = jnp.where(far, lax.rem(m, cross), cross + k // nc)
         c = jnp.where(far, m // cross, lax.rem(k, nc))
 
-        @pl.when(jnp.logical_and(far, s == 0))
+        @pl.when(jnp.logical_and(far, jnp.logical_and(s == 0, c >= deep)))
         def _():
             wait_edges(c, cross * q)
 
-        @pl.when(jnp.logical_and(jnp.logical_not(far), c == 0))
-        def _():
-            wait_edges(nc + s - cross, per)
-
-        advance(s, c, put_adv)
-
-        @pl.when(m != cross * nc - 1)
-        def _():
-            block_copy(s, c).start()
+        @pl.when(jnp.logical_not(far))
+        def _():
+            wait_edges(nc + k, q)
+
+        @pl.when(jnp.logical_or(s > 0, c >= deep))
+        def _():
+            advance(s, c, put_adv)
+
+            @pl.when(m != cross * nc - 1)
+            def _():
+                block_copy(s, c).start()
 
         return carry
 
-    lax.fori_loop(early * cross, (ranks - 1) * nc, away_step, 0)
+    lax.fori_loop(cross, (ranks - 1) * nc, away_step, 0)
+
+    @pl.when(jnp.logical_not(late))
+    def _():
+        giver = lax.rem(a + chips - 1, chips) * cores
+
+        def put_given(t, lev, kept, c):
+            cells[giver * nt + t, 0, kept] = c
+
+        pltpu.make_async_copy(raw, raw, r_recv.at[0]).wait()
+        advect(
+            r * per, r, PAD, rows, EDGE, EDGE, rows - 2 * EDGE, put_given,
+            lambda t: raw[t], giver,
+        )
 
     def own_step(c, carry):
+        wait_edges(cores * nc + c, q)
         advance(ranks - 1, c, put_cells)
         return carry
 
-    wait_edges(nc + cores - 1, per)
     lax.fori_loop(0, nc, own_step, 0)
 
     above = jnp.zeros((rows, width), jnp.float32)
@@ -521,7 +564,13 @@
         aux[0] = (above + clear) * scale
 
     def react_chunk(c, carry):
-        wait_blocks(c)
+        @pl.when(c == 0)
+        def _():
+            wait_first()
+
+        @pl.when(c > 0)
+        def _():
+            wait_blocks(c)
 
         def one_level(j, carry):
             i = c * q + j
@@ -552,7 +601,17 @@
         def _():
             over_copy(k).wait_send()
 
-    settle(adv.at[:, pl.ds(0, (ranks - 1) * per)], d_send.at[0])
+    settle(adv.at[:, pl.ds(0, (ranks - 1) * per - early * q)], d_send.at[0])
+    settle(ext.at[:, pl.ds(0, early * q), pl.ds(0, 2 * EDGE)], d_send.at[2])
+    for pieces, mask in ((early * q, late), (early * q - 1, jnp.logical_not(late))):
+        @pl.when(mask)
+        def _():
+            settle(ext.at[:, pl.ds(0, pieces), inner], d_send.at[1])
+
+    @pl.when(jnp.logical_not(late))
+    def _():
+        raw_copy().wait_send()
+
     wait_blocks(nc - 1)
 
 
@@ -628,14 +687,14 @@
         count = ranks * nt
         cross = ranks - cores
         chips = ranks // cores
-        early = min(2, nc - 1)
+        deep = min(DEEP, nc - 1)
         full = rows + PAD
         f32 = jnp.float32
         any_space = pl.BlockSpec(memory_space=pl.ANY)
         vmem = pl.BlockSpec(memory_space=pltpu.VMEM)
         dma = pltpu.SemaphoreType.DMA
         cells, vel, heat, aux = pl.pallas_call(
-            functools.partial(transport_kernel, tiles, ranks, cores, q, early),
+            functools.partial(transport_kernel, tiles, ranks, cores, q, deep),
             out_shape=(
                 pltpu.VMEM((count, per, rows, width), f32),
                 pltpu.VMEM((2, per, rows, width), f32),
@@ -661,10 +720,11 @@
                 pltpu.VMEM((count, rows, width), f32),
                 pltpu.VMEM((count, rows, width), f32),
                 pltpu.SMEM((count,), jnp.int32),
-                dma((4,)), dma((nc + cores,)), dma((nc + cores,)), dma((2,)),
-                dma((1,)), dma((nc,)), dma((chips,)), dma((chips,)),
-                dma((early * cross + 1,)), dma((2,)), dma((3,)), dma((3,)),
-                pltpu.SemaphoreType.REGULAR,
+                pltpu.VMEM((nt, rows, width), f32),
+                dma((4,)), dma((nc + cores * nc,)), dma((nc + cores * nc,)), dma((2,)),
+                dma((3,)), dma((nc + 1,)), dma((chips,)), dma((chips,)),
+                dma((deep + cross,)), dma((2,)), dma((3,)), dma((3,)),
+                dma((1,)), dma((1,)), pltpu.SemaphoreType.REGULAR,
             ],
             compiler_params=pltpu.CompilerParams(
                 collective_id=0, has_side_effects=True, vmem_limit_bytes=48 << 20

time: 54.1 us -> 53.3 us (0.985)
  the two profiles are of different devices: /device:TPU:1 before, /device:TPU:0 now
where the time goes in v7:
time: 53.3 us; the launch traced here: 52.4 us
  Pallas kernels  51.7 us (97%)
  between operations  0.69 us (1%)
    pallas_call x1, Pallas kernels, on_device(): pl.pallas_call(functools.partial(transport_kernel, tiles, ranks, cores, q...  49.5 us
    pallas_call x1, Pallas kernels, on_device(): pl.pallas_call(functools.partial(finish_kernel, nl, q), out_shape=(jax.Sh...  2.2 us

profile of v7, /device:TPU:0, one launch (start us, length us, event | category | flops | bytes accessed | tf_op | source)
XLA Modules:
  0.0 52.4 jit_solution(593909216924408359)
XLA Ops:
  0.6 0.0 copy-start.2
  0.6 0.0 copy-start.1
  0.7 0.0 copy-start
  0.7 49.5 %transport.1 = (f32[32,8,32,128]{3,2,1,0:T(8,128)S(1)}, f32[2,8,32,128]{3,2,1,0:T(8,128)S(1)}, f32[8,32,128]{2,1,0:T(8,128)S(1)}, f32[3,32,128]{2,1,0:T(8,128)S(1)}) custom-call(f32[8,32,32,128]{3,2,1,0:T(8,128)} %sp.1, f32[2,32,32,128]{3,2,1,0:T(8,128)} %fc.1, f32[8,32,128]{2,1,0:T(8,128)} %th.1, s32[32,128]{1,0:T(8,128)} %dep.1, f32[32,128]{1,0:T(8,128)} %sun.1, ...), custom_call_target="tpu_custom_call" | custom-call | tf_op jit(solution)/shard_map/transport/pallas_call | solution.py:696
  50.2 0.0 copy-done.2
  50.2 0.0 copy-done.1
  50.2 0.0 copy-done
  50.2 2.2 %finish.1 = (f32[32,8,32,128]{3,2,1,0:T(8,128)}, f32[2,8,32,128]{3,2,1,0:T(8,128)}, f32[8,32,128]{2,1,0:T(8,128)}) custom-call(f32[32,8,32,128]{3,2,1,0:T(8,128)S(1)} %get-tuple-element.7.cells, f32[2,8,32,128]{3,2,1,0:T(8,128)S(1)} %get-tuple-element.8.vel, f32[8,32,128]{2,1,0:T(8,128)S(1)} %get-tuple-element.9.heat, ...), custom_call_target="tpu_custom_call" | custom-call | tf_op jit(solution)/shard_map/finish/pallas_call | solution.py:740
Async XLA Ops:
  0.6 49.5 %copy-start.2 = (f32[32]{0:T(128)S(1)}, f32[32]{0:T(128)}, u32[]{:S(2)}) copy-start(f32[32]{0:T(128)} %rate_in.3) | copy-start | bytes 388
  0.6 49.5 %copy-start.1 = (f32[32]{0:T(128)S(1)}, f32[32]{0:T(128)}, u32[]{:S(2)}) copy-start(f32[32]{0:T(128)} %att_in.3) | copy-start | bytes 388
  0.7 49.5 %copy-start = (s32[32]{0:T(128)S(1)}, s32[32]{0:T(128)}, u32[]{:S(2)}) copy-start(s32[32]{0:T(128)} %eaten_in.3) | copy-start | bytes 388

commit v8 on v7

--- a/solution.py
+++ b/solution.py
@@ -26,7 +26,7 @@
 EDGE = 4
 TILE = 8
 LOW_FLOW, HIGH_FLOW = 3, 2
-DEEP = 3
+DEEP = 2
 
 HBM = pltpu.HBM
 
@@ -96,7 +96,7 @@
     sp, fc, th, dep, sun, eaten_in, att_in, rate_in,
     cells, vel, heat, aux,
     eaten, att, rate, ext, fext, hext, dext, adv, tot, pre, part, joined, over, sat, pull, eater, raw,
-    edge_send, h_recv, f_recv, s_recv, d_send, d_recv, o_send, o_recv,
+    edge_send, g_recv, s_recv, d_send, d_recv, o_send, o_recv,
     l_sem, lf_sem, ls_sem, t_sem, r_send, r_recv, ready,
 ):
     nt, nl, rows, width = sp.shape
@@ -143,22 +143,26 @@
         )
 
     def edges(s, c):
-        g = jnp.where(s < cross, c, nc + (s - cross) * nc + c)
+        g = jnp.where(s < cross, c, jnp.where(s < ranks - 1, nc + s - cross, own_group + c))
         lead = (slice(None), pl.ds(first_level(s, c), q))
         return (
-            pair(fc, fext, lead, edge_send.at[0], f_recv.at[g], LOW_FLOW, HIGH_FLOW)
-            + pair(sp, ext, lead, edge_send.at[1], h_recv.at[g])
-        )
+            pair(fc, fext, lead, edge_send.at[0], g_recv.at[g], LOW_FLOW, HIGH_FLOW)
+            + pair(sp, ext, lead, edge_send.at[0], g_recv.at[g])
+        )
+
+    own_group = nc + cores - 1
+
+    def edge_rows(levels):
+        return fext.at[:, pl.ds(0, levels), pl.ds(0, nt * EDGE + LOW_FLOW + HIGH_FLOW)]
 
     def wait_edges(g, levels):
-        settle(fext.at[:, pl.ds(0, levels), pl.ds(0, LOW_FLOW + HIGH_FLOW)], f_recv.at[g])
-        settle(ext.at[:, pl.ds(0, levels), pl.ds(0, 2 * EDGE)], h_recv.at[g])
+        settle(edge_rows(levels), g_recv.at[g])
 
     def heat_edges():
-        return pair(th, hext, (slice(None),), edge_send.at[2], s_recv.at[0])
+        return pair(th, hext, (slice(None),), edge_send.at[1], s_recv.at[0])
 
     def depth_edges():
-        return pair(dep, dext, (), edge_send.at[3], s_recv.at[1])
+        return pair(dep, dext, (), edge_send.at[2], s_recv.at[1])
 
     def flow_local(s):
         lev = pl.ds(target(s) * per, per)
@@ -196,26 +200,30 @@
             device_id={"tracer": target(s)}, device_id_type=MESH,
         )
 
-    def outer_copy(s, c, side):
+    def outer_copy(s, c, side, skip=0):
         edge = pl.ds(side * (rows - EDGE), EDGE)
         return pltpu.make_async_remote_copy(
-            adv.at[:, pl.ds(first_level(s, c), q), edge],
-            cells.at[mine, pl.ds(c * q, q), edge],
+            adv.at[:, pl.ds(first_level(s, c) + skip, q - skip), edge],
+            cells.at[mine, pl.ds(c * q + skip, q - skip), edge],
             d_send.at[2], d_recv.at[c],
             device_id={"tracer": target(s)}, device_id_type=MESH,
         )
 
     def raw_copy():
         return pltpu.make_async_remote_copy(
-            sp.at[:, first_level(0, 0)], raw, r_send.at[0], r_recv.at[0],
+            sp.at[:, first_level(0, 0)], raw.at[:, body], r_send.at[0], r_recv.at[0],
             device_id={"tracer": target(0)}, device_id_type=MESH,
         )
 
+    def raw_edges():
+        return pair(raw.at[:, body], raw, (slice(None),), r_send.at[1], r_recv.at[1])
+
     def wait_first():
-        settle(ext.at[:, pl.ds(0, q * (cross + rows // TILE)), pl.ds(0, TILE)], d_recv.at[0])
         for pieces, mask in ((cross * q, late), (cross * q - 1, jnp.logical_not(late))):
             @pl.when(mask)
             def _():
+                strips = pl.ds(0, pieces + q * (rows // TILE))
+                settle(ext.at[:, strips, pl.ds(0, TILE)], d_recv.at[0])
                 settle(ext.at[:, pl.ds(0, pieces), inner], d_recv.at[nc])
 
     def wait_blocks(c):
@@ -248,8 +256,6 @@
     last_core = a * cores + cores - 1
     late = b == cores - 1
     barrier = pltpu.get_barrier_semaphore()
-    for s in range(cores - 1, cross, cores):
-        pl.semaphore_signal(barrier, inc=1, device_id={"tracer": target(s)}, device_id_type=MESH)
     if cores > 1:
         @pl.when(jnp.logical_not(late))
         def _():
@@ -262,6 +268,8 @@
         pl.semaphore_signal(
             barrier, inc=1, device_id={"tile": place, "tracer": last_core}, device_id_type=MESH
         )
+    for s in range(cores - 1, cross, cores):
+        pl.semaphore_signal(barrier, inc=1, device_id={"tracer": target(s)}, device_id_type=MESH)
 
     dep_local = pltpu.make_async_copy(dep, dext.at[body], ls_sem.at[0])
     th_local = pltpu.make_async_copy(th, hext.at[:, body], ls_sem.at[1])
@@ -279,14 +287,15 @@
         early_local(k).start()
         return carry
 
-    lax.fori_loop(0, early, start_early, 0)
-    for s in range(1, ranks):
-        flow_local(s).start()
-
+    early_local(0).start()
     @pl.when(jnp.logical_not(late))
     def _():
         pl.semaphore_wait(barrier, chips - 1)
         raw_copy().start()
+
+    lax.fori_loop(1, early, start_early, 0)
+    for s in range(1, ranks):
+        flow_local(s).start()
 
     tot[...] = jnp.zeros_like(tot)
     dep_local.wait()
@@ -413,6 +422,13 @@
     lax.fori_loop(cross, cross * nc, start_edges(in_cross), 0)
     for s in range(ranks):
         rest_local(s).start()
+
+    @pl.when(jnp.logical_not(late))
+    def _():
+        raw_copy().wait_recv()
+        for copy in raw_edges():
+            copy.start()
+
     lax.fori_loop(0, cores * nc, start_edges(in_near), 0)
     for copy in heat_edges():
         copy.start()
@@ -420,6 +436,18 @@
     sun_local.start()
     tables[0].start()
     tables[2].start()
+    tables[0].wait()
+    tables[2].wait()
+
+    def invert(s, carry):
+        who = jnp.int32(0)
+        for t in range(count):
+            who = jnp.where(eaten[t] == s, jnp.int32(t), who)
+        eater[s] = who
+        return carry
+
+    lax.fori_loop(0, count, invert, 0)
+
     settle(dext.at[pl.ds(0, 2 * EDGE)], s_recv.at[1])
 
     def outer_step(k, carry):
@@ -433,9 +461,20 @@
             advance_outer(s, c, i)
             return carry
 
-        lax.fori_loop(0, q, sides, 0)
-        for side in range(2):
-            outer_copy(s, c, side).start()
+        given = jnp.logical_and(jnp.logical_not(late), k == 0)
+        lax.fori_loop(jnp.where(given, 1, 0), q, sides, 0)
+
+        @pl.when(jnp.logical_not(given))
+        def _():
+            for side in range(2):
+                outer_copy(s, c, side).start()
+
+        if q > 1:
+            @pl.when(given)
+            def _():
+                for side in range(2):
+                    outer_copy(s, c, side, 1).start()
+
         return carry
 
     lax.fori_loop(0, early, outer_step, 0)
@@ -452,9 +491,9 @@
         def _():
             wait_edges(c, cross * q)
 
-        @pl.when(jnp.logical_not(far))
-        def _():
-            wait_edges(nc + k, q)
+        @pl.when(jnp.logical_and(jnp.logical_not(far), c == 0))
+        def _():
+            wait_edges(nc + s - cross, per)
 
         @pl.when(jnp.logical_or(s > 0, c >= deep))
         def _():
@@ -468,6 +507,8 @@
 
     lax.fori_loop(cross, (ranks - 1) * nc, away_step, 0)
 
+    wait_edges(own_group, q)
+
     @pl.when(jnp.logical_not(late))
     def _():
         giver = lax.rem(a + chips - 1, chips) * cores
@@ -475,14 +516,14 @@
         def put_given(t, lev, kept, c):
             cells[giver * nt + t, 0, kept] = c
 
-        pltpu.make_async_copy(raw, raw, r_recv.at[0]).wait()
-        advect(
-            r * per, r, PAD, rows, EDGE, EDGE, rows - 2 * EDGE, put_given,
-            lambda t: raw[t], giver,
-        )
+        settle(raw.at[:, pl.ds(0, 2 * EDGE)], r_recv.at[1])
+        advect(r * per, r, 0, full, PAD, 0, rows, put_given, lambda t: raw[t], giver)
 
     def own_step(c, carry):
-        wait_edges(cores * nc + c, q)
+        @pl.when(c > 0)
+        def _():
+            wait_edges(own_group + c, q)
+
         advance(ranks - 1, c, put_cells)
         return carry
 
@@ -534,18 +575,6 @@
 
     lax.fori_loop(0, per, momentum, 0)
 
-    tables[0].wait()
-    tables[2].wait()
-
-    def invert(s, carry):
-        who = jnp.int32(0)
-        for t in range(count):
-            who = jnp.where(eaten[t] == s, jnp.int32(t), who)
-        eater[s] = who
-        return carry
-
-    lax.fori_loop(0, count, invert, 0)
-
     depth = dext[PAD:PAD + rows].astype(jnp.float32)
     aux[2] = depth
     scale = column_optical / nl
@@ -592,25 +621,25 @@
 
     lax.fori_loop(0, nc - 1, react_chunk, 0)
 
-    settle(fc.at[:, :, pl.ds(0, LOW_FLOW + HIGH_FLOW)], edge_send.at[0])
-    settle(sp.at[:, :, pl.ds(0, 2 * EDGE)], edge_send.at[1])
-    settle(th.at[:, pl.ds(0, 2 * EDGE)], edge_send.at[2])
-    settle(dep.at[pl.ds(0, 2 * EDGE)], edge_send.at[3])
+    settle(edge_rows(nl), edge_send.at[0])
+    settle(th.at[:, pl.ds(0, 2 * EDGE)], edge_send.at[1])
+    settle(dep.at[pl.ds(0, 2 * EDGE)], edge_send.at[2])
     for k in range(1, chips):
         @pl.when(gets_over(k))
         def _():
             over_copy(k).wait_send()
 
     settle(adv.at[:, pl.ds(0, (ranks - 1) * per - early * q)], d_send.at[0])
-    settle(ext.at[:, pl.ds(0, early * q), pl.ds(0, 2 * EDGE)], d_send.at[2])
     for pieces, mask in ((early * q, late), (early * q - 1, jnp.logical_not(late))):
         @pl.when(mask)
         def _():
+            settle(ext.at[:, pl.ds(0, pieces), pl.ds(0, 2 * EDGE)], d_send.at[2])
             settle(ext.at[:, pl.ds(0, pieces), inner], d_send.at[1])
 
     @pl.when(jnp.logical_not(late))
     def _():
         raw_copy().wait_send()
+        settle(raw.at[:, pl.ds(0, 2 * EDGE)], r_send.at[1])
 
     wait_blocks(nc - 1)
 
@@ -720,11 +749,11 @@
                 pltpu.VMEM((count, rows, width), f32),
                 pltpu.VMEM((count, rows, width), f32),
                 pltpu.SMEM((count,), jnp.int32),
-                pltpu.VMEM((nt, rows, width), f32),
-                dma((4,)), dma((nc + cores * nc,)), dma((nc + cores * nc,)), dma((2,)),
+                pltpu.VMEM((nt, full, width), f32),
+                dma((3,)), dma((2 * nc + cores - 1,)), dma((2,)),
                 dma((3,)), dma((nc + 1,)), dma((chips,)), dma((chips,)),
                 dma((deep + cross,)), dma((2,)), dma((3,)), dma((3,)),
-                dma((1,)), dma((1,)), pltpu.SemaphoreType.REGULAR,
+                dma((2,)), dma((2,)), pltpu.SemaphoreType.REGULAR,
             ],
             compiler_params=pltpu.CompilerParams(
                 collective_id=0, has_side_effects=True, vmem_limit_bytes=48 << 20

time: 53.3 us -> 52.8 us (level); the launches traced: 52.4 us -> 52.7 us
  no operation moved by 1% of the time
where the time goes in v8:
time: 52.8 us; the launch traced here: 52.7 us
  Pallas kernels  52 us (98%)
  between operations  0.69 us (1%)
    pallas_call x1, Pallas kernels, on_device(): pl.pallas_call(functools.partial(transport_kernel, tiles, ranks, cores, q...  49.8 us
    pallas_call x1, Pallas kernels, on_device(): pl.pallas_call(functools.partial(finish_kernel, nl, q), out_shape=(jax.Sh...  2.2 us

profile of v8, /device:TPU:0, one launch (start us, length us, event | category | flops | bytes accessed | tf_op | source)
XLA Modules:
  0.0 52.7 jit_solution(17605058146181815316)
XLA Ops:
  0.6 0.0 copy-start.2
  0.6 0.0 copy-start.1
  0.7 0.0 copy-start
  0.7 49.8 %transport.1 = (f32[32,8,32,128]{3,2,1,0:T(8,128)S(1)}, f32[2,8,32,128]{3,2,1,0:T(8,128)S(1)}, f32[8,32,128]{2,1,0:T(8,128)S(1)}, f32[3,32,128]{2,1,0:T(8,128)S(1)}) custom-call(f32[8,32,32,128]{3,2,1,0:T(8,128)} %sp.1, f32[2,32,32,128]{3,2,1,0:T(8,128)} %fc.1, f32[8,32,128]{2,1,0:T(8,128)} %th.1, s32[32,128]{1,0:T(8,128)} %dep.1, f32[32,128]{1,0:T(8,128)} %sun.1, ...), custom_call_target="tpu_custom_call" | custom-call | tf_op jit(solution)/shard_map/transport/pallas_call | solution.py:725
  50.5 0.0 copy-done.2
  50.5 0.0 copy-done.1
  50.5 0.0 copy-done
  50.5 2.2 %finish.1 = (f32[32,8,32,128]{3,2,1,0:T(8,128)}, f32[2,8,32,128]{3,2,1,0:T(8,128)}, f32[8,32,128]{2,1,0:T(8,128)}) custom-call(f32[32,8,32,128]{3,2,1,0:T(8,128)S(1)} %get-tuple-element.7.cells, f32[2,8,32,128]{3,2,1,0:T(8,128)S(1)} %get-tuple-element.8.vel, f32[8,32,128]{2,1,0:T(8,128)S(1)} %get-tuple-element.9.heat, ...), custom_call_target="tpu_custom_call" | custom-call | tf_op jit(solution)/shard_map/finish/pallas_call | solution.py:769
Async XLA Ops:
  0.6 49.8 %copy-start.2 = (f32[32]{0:T(128)S(1)}, f32[32]{0:T(128)}, u32[]{:S(2)}) copy-start(f32[32]{0:T(128)} %rate_in.3) | copy-start | bytes 388
  0.6 49.8 %copy-start.1 = (f32[32]{0:T(128)S(1)}, f32[32]{0:T(128)}, u32[]{:S(2)}) copy-start(f32[32]{0:T(128)} %att_in.3) | copy-start | bytes 388
  0.7 49.8 %copy-start = (s32[32]{0:T(128)S(1)}, s32[32]{0:T(128)}, u32[]{:S(2)}) copy-start(s32[32]{0:T(128)} %eaten_in.3) | copy-start | bytes 388

commit v9 on v8

--- a/solution.py
+++ b/solution.py
@@ -196,7 +196,7 @@
         return pltpu.make_async_remote_copy(
             adv.at[:, first_level(s, c) + i, inner],
             cells.at[mine, c * q + i, inner],
-            d_send.at[1], d_recv.at[jnp.where(c == 0, nc, c)],
+            d_send.at[0], d_recv.at[c],
             device_id={"tracer": target(s)}, device_id_type=MESH,
         )
 
@@ -205,7 +205,7 @@
         return pltpu.make_async_remote_copy(
             adv.at[:, pl.ds(first_level(s, c) + skip, q - skip), edge],
             cells.at[mine, pl.ds(c * q + skip, q - skip), edge],
-            d_send.at[2], d_recv.at[c],
+            d_send.at[0], d_recv.at[c],
             device_id={"tracer": target(s)}, device_id_type=MESH,
         )
 
@@ -216,15 +216,13 @@
         )
 
     def raw_edges():
-        return pair(raw.at[:, body], raw, (slice(None),), r_send.at[1], r_recv.at[1])
+        return pair(raw.at[:, body], raw, (slice(None),), r_send.at[0], r_recv.at[1])
 
     def wait_first():
-        for pieces, mask in ((cross * q, late), (cross * q - 1, jnp.logical_not(late))):
+        for given, mask in ((0, late), (1, jnp.logical_not(late))):
             @pl.when(mask)
             def _():
-                strips = pl.ds(0, pieces + q * (rows // TILE))
-                settle(ext.at[:, strips, pl.ds(0, TILE)], d_recv.at[0])
-                settle(ext.at[:, pl.ds(0, pieces), inner], d_recv.at[nc])
+                settle(adv.at[:, pl.ds(0, (ranks - 1) * q - given)], d_recv.at[0])
 
     def wait_blocks(c):
         settle(cells.at[pl.ds(0, (ranks - 1) * nt), pl.ds(c * q, q)], d_recv.at[c])
@@ -529,28 +527,6 @@
 
     lax.fori_loop(0, nc, own_step, 0)
 
-    above = jnp.zeros((rows, width), jnp.float32)
-    for place in range(ranks):
-        pre[place // cores, place % cores] = above
-        above = above + tot[place]
-    if cores > 1:
-        part_copy().start()
-        part_copy().wait()
-        for k in range(chips):
-            joined[k] = pre[k, b] + part[k]
-    else:
-        for k in range(chips):
-            joined[k] = pre[k, b]
-    for k in range(1, chips):
-        @pl.when(gets_over(k))
-        def _():
-            over_copy(k).start()
-
-    block_copy(cross - 1, nc - 1).start()
-
-    th_local.wait()
-    sun_local.wait()
-    settle(hext.at[:, pl.ds(0, 2 * EDGE)], s_recv.at[0])
     lane = lane_index((full, width))
     coriolis = coriolis_base + beta_plane * lane.astype(jnp.float32) / width
 
@@ -573,7 +549,39 @@
         heat[i] = warmer[PAD:PAD + rows]
         return carry
 
-    lax.fori_loop(0, per, momentum, 0)
+    def move():
+        th_local.wait()
+        sun_local.wait()
+        settle(hext.at[:, pl.ds(0, 2 * EDGE)], s_recv.at[0])
+        lax.fori_loop(0, per, momentum, 0)
+
+    above = jnp.zeros((rows, width), jnp.float32)
+    for place in range(ranks):
+        pre[place // cores, place % cores] = above
+        above = above + tot[place]
+    if cores > 1:
+        part_copy().start()
+
+        @pl.when(jnp.logical_not(late))
+        def _():
+            move()
+
+        part_copy().wait()
+        for k in range(chips):
+            joined[k] = pre[k, b] + part[k]
+    else:
+        for k in range(chips):
+            joined[k] = pre[k, b]
+    for k in range(1, chips):
+        @pl.when(gets_over(k))
+        def _():
+            over_copy(k).start()
+
+    block_copy(cross - 1, nc - 1).start()
+
+    @pl.when(late)
+    def _():
+        move()
 
     depth = dext[PAD:PAD + rows].astype(jnp.float32)
     aux[2] = depth
@@ -629,17 +637,14 @@
         def _():
             over_copy(k).wait_send()
 
-    settle(adv.at[:, pl.ds(0, (ranks - 1) * per - early * q)], d_send.at[0])
-    for pieces, mask in ((early * q, late), (early * q - 1, jnp.logical_not(late))):
+    for given, mask in ((0, late), (1, jnp.logical_not(late))):
         @pl.when(mask)
         def _():
-            settle(ext.at[:, pl.ds(0, pieces), pl.ds(0, 2 * EDGE)], d_send.at[2])
-            settle(ext.at[:, pl.ds(0, pieces), inner], d_send.at[1])
+            settle(adv.at[:, pl.ds(0, (ranks - 1) * per - given)], d_send.at[0])
 
     @pl.when(jnp.logical_not(late))
     def _():
-        raw_copy().wait_send()
-        settle(raw.at[:, pl.ds(0, 2 * EDGE)], r_send.at[1])
+        settle(raw, r_send.at[0])
 
     wait_blocks(nc - 1)
 
@@ -657,7 +662,7 @@
     copies = [
         pltpu.make_async_copy(cells.at[:, pl.ds(0, done)], out.at[:, pl.ds(0, done)], sem.at[0]),
         pltpu.make_async_copy(vel, vel_out, sem.at[1]),
-        pltpu.make_async_copy(heat.at[pl.ds(0, done)], temp_out.at[pl.ds(0, done)], sem.at[2]),
+        pltpu.make_async_copy(heat.at[pl.ds(0, done)], temp_out.at[pl.ds(0, done)], sem.at[1]),
     ]
     tables = [
         pltpu.make_async_copy(src, dst, t_sem.at[k])
@@ -671,7 +676,7 @@
         eater[eaten[t]] = t
 
     def level_copy(j):
-        return pltpu.make_async_copy(last.at[j], out.at[:, done + j], sem.at[4])
+        return pltpu.make_async_copy(last.at[j], out.at[:, done + j], sem.at[0])
 
     def one_level(j, tau):
         def put(t, x):
@@ -687,12 +692,11 @@
         return below
 
     lax.fori_loop(0, q, one_level, aux[0])
-    warm_copy = pltpu.make_async_copy(warm, temp_out.at[pl.ds(done, q)], sem.at[3])
+    warm_copy = pltpu.make_async_copy(warm, temp_out.at[pl.ds(done, q)], sem.at[1])
     warm_copy.start()
-    for copy in copies:
-        copy.wait()
-    pltpu.make_async_copy(last, last, sem.at[4]).wait()
-    warm_copy.wait()
+    flows = cells.at[pl.ds(0, 3 * per), 0]
+    pltpu.make_async_copy(cells, cells, sem.at[0]).wait()
+    pltpu.make_async_copy(flows, flows, sem.at[1]).wait()
 
 
 def solution(mesh):
@@ -751,9 +755,9 @@
                 pltpu.SMEM((count,), jnp.int32),
                 pltpu.VMEM((nt, full, width), f32),
                 dma((3,)), dma((2 * nc + cores - 1,)), dma((2,)),
-                dma((3,)), dma((nc + 1,)), dma((chips,)), dma((chips,)),
+                dma((1,)), dma((nc,)), dma((chips,)), dma((chips,)),
                 dma((deep + cross,)), dma((2,)), dma((3,)), dma((3,)),
-                dma((2,)), dma((2,)), pltpu.SemaphoreType.REGULAR,
+                dma((1,)), dma((2,)), pltpu.SemaphoreType.REGULAR,
             ],
             compiler_params=pltpu.CompilerParams(
                 collective_id=0, has_side_effects=True, vmem_limit_bytes=48 << 20
@@ -784,7 +788,7 @@
                 pltpu.VMEM((count, rows, width), f32),
                 pltpu.VMEM((count, rows, width), f32),
                 pltpu.SMEM((count,), jnp.int32),
-                dma((5,)), dma((3,)),
+                dma((2,)), dma((3,)),
             ],
             compiler_params=pltpu.CompilerParams(vmem_limit_bytes=32 << 20),
             name="finish",

time: 52.8 us -> 52.8 us (level)
  no operation moved by 1% of the time
where the time goes in v9:
time: 52.8 us; the launch traced here: 52.7 us
  Pallas kernels  52 us (98%)
  between operations  0.69 us (1%)
    pallas_call x1, Pallas kernels, on_device(): pl.pallas_call(functools.partial(transport_kernel, tiles, ranks, cores, q...  49.8 us
    pallas_call x1, Pallas kernels, on_device(): pl.pallas_call(functools.partial(finish_kernel, nl, q), out_shape=(jax.Sh...  2.17 us

profile of v9, /device:TPU:0, one launch (start us, length us, event | category | flops | bytes accessed | tf_op | source)
XLA Modules:
  0.0 52.7 jit_solution(4413470890705622209)
XLA Ops:
  0.6 0.0 copy-start.2
  0.6 0.0 copy-start.1
  0.7 0.0 copy-start
  0.7 49.8 %transport.1 = (f32[32,8,32,128]{3,2,1,0:T(8,128)S(1)}, f32[2,8,32,128]{3,2,1,0:T(8,128)S(1)}, f32[8,32,128]{2,1,0:T(8,128)S(1)}, f32[3,32,128]{2,1,0:T(8,128)S(1)}) custom-call(f32[8,32,32,128]{3,2,1,0:T(8,128)} %sp.1, f32[2,32,32,128]{3,2,1,0:T(8,128)} %fc.1, f32[8,32,128]{2,1,0:T(8,128)} %th.1, s32[32,128]{1,0:T(8,128)} %dep.1, f32[32,128]{1,0:T(8,128)} %sun.1, ...), custom_call_target="tpu_custom_call" | custom-call | tf_op jit(solution)/shard_map/transport/pallas_call | solution.py:729
  50.5 0.0 copy-done.2
  50.5 0.0 copy-done.1
  50.5 0.0 copy-done
  50.5 2.2 %finish.1 = (f32[32,8,32,128]{3,2,1,0:T(8,128)}, f32[2,8,32,128]{3,2,1,0:T(8,128)}, f32[8,32,128]{2,1,0:T(8,128)}) custom-call(f32[32,8,32,128]{3,2,1,0:T(8,128)S(1)} %get-tuple-element.7.cells, f32[2,8,32,128]{3,2,1,0:T(8,128)S(1)} %get-tuple-element.8.vel, f32[8,32,128]{2,1,0:T(8,128)S(1)} %get-tuple-element.9.heat, ...), custom_call_target="tpu_custom_call" | custom-call | tf_op jit(solution)/shard_map/finish/pallas_call | solution.py:773
Async XLA Ops:
  0.6 49.8 %copy-start.2 = (f32[32]{0:T(128)S(1)}, f32[32]{0:T(128)}, u32[]{:S(2)}) copy-start(f32[32]{0:T(128)} %rate_in.3) | copy-start | bytes 388
  0.6 49.8 %copy-start.1 = (f32[32]{0:T(128)S(1)}, f32[32]{0:T(128)}, u32[]{:S(2)}) copy-start(f32[32]{0:T(128)} %att_in.3) | copy-start | bytes 388
  0.7 49.8 %copy-start = (s32[32]{0:T(128)S(1)}, s32[32]{0:T(128)}, u32[]{:S(2)}) copy-start(s32[32]{0:T(128)} %eaten_in.3) | copy-start | bytes 388

commit v10 on v8

--- a/solution.py
+++ b/solution.py
@@ -481,6 +481,8 @@
 
     settle(ext.at[:, pl.ds(0, nl - early * q), body], l_sem.at[early])
 
+    holds = functools.reduce(jnp.logical_or, [gets_over(k) for k in range(1, chips)])
+
     def away_step(m, carry):
         far = m < cross * nc
         k = m - cross * nc
@@ -499,7 +501,7 @@
         def _():
             advance(s, c, put_adv)
 
-            @pl.when(m != cross * nc - 1)
+            @pl.when(jnp.logical_or(m != cross * nc - 1, jnp.logical_not(holds)))
             def _():
                 block_copy(s, c).start()
 
@@ -546,7 +548,9 @@
         def _():
             over_copy(k).start()
 
-    block_copy(cross - 1, nc - 1).start()
+    @pl.when(holds)
+    def _():
+        block_copy(cross - 1, nc - 1).start()
 
     th_local.wait()
     sun_local.wait()

time: 52.8 us -> 52.8 us (level)
  no operation moved by 1% of the time
where the time goes in v10:
time: 52.8 us; the launch traced here: 52.7 us
  Pallas kernels  52 us (98%)
  between operations  0.69 us (1%)
    pallas_call x1, Pallas kernels, on_device(): pl.pallas_call(functools.partial(transport_kernel, tiles, ranks, cores, q...  49.8 us
    pallas_call x1, Pallas kernels, on_device(): pl.pallas_call(functools.partial(finish_kernel, nl, q), out_shape=(jax.Sh...  2.2 us

profile of v10, /device:TPU:0, one launch (start us, length us, event | category | flops | bytes accessed | tf_op | source)
XLA Modules:
  0.0 52.7 jit_solution(10774126990888231391)
XLA Ops:
  0.6 0.0 copy-start.2
  0.6 0.0 copy-start.1
  0.7 0.0 copy-start
  0.7 49.8 %transport.1 = (f32[32,8,32,128]{3,2,1,0:T(8,128)S(1)}, f32[2,8,32,128]{3,2,1,0:T(8,128)S(1)}, f32[8,32,128]{2,1,0:T(8,128)S(1)}, f32[3,32,128]{2,1,0:T(8,128)S(1)}) custom-call(f32[8,32,32,128]{3,2,1,0:T(8,128)} %sp.1, f32[2,32,32,128]{3,2,1,0:T(8,128)} %fc.1, f32[8,32,128]{2,1,0:T(8,128)} %th.1, s32[32,128]{1,0:T(8,128)} %dep.1, f32[32,128]{1,0:T(8,128)} %sun.1, ...), custom_call_target="tpu_custom_call" | custom-call | tf_op jit(solution)/shard_map/transport/pallas_call | solution.py:729
  50.5 0.0 copy-done.2
  50.5 0.0 copy-done.1
  50.5 0.0 copy-done
  50.5 2.2 %finish.1 = (f32[32,8,32,128]{3,2,1,0:T(8,128)}, f32[2,8,32,128]{3,2,1,0:T(8,128)}, f32[8,32,128]{2,1,0:T(8,128)}) custom-call(f32[32,8,32,128]{3,2,1,0:T(8,128)S(1)} %get-tuple-element.7.cells, f32[2,8,32,128]{3,2,1,0:T(8,128)S(1)} %get-tuple-element.8.vel, f32[8,32,128]{2,1,0:T(8,128)S(1)} %get-tuple-element.9.heat, ...), custom_call_target="tpu_custom_call" | custom-call | tf_op jit(solution)/shard_map/finish/pallas_call | solution.py:773
Async XLA Ops:
  0.6 49.8 %copy-start.2 = (f32[32]{0:T(128)S(1)}, f32[32]{0:T(128)}, u32[]{:S(2)}) copy-start(f32[32]{0:T(128)} %rate_in.3) | copy-start | bytes 388
  0.6 49.8 %copy-start.1 = (f32[32]{0:T(128)S(1)}, f32[32]{0:T(128)}, u32[]{:S(2)}) copy-start(f32[32]{0:T(128)} %att_in.3) | copy-start | bytes 388
  0.7 49.8 %copy-start = (s32[32]{0:T(128)S(1)}, s32[32]{0:T(128)}, u32[]{:S(2)}) copy-start(s32[32]{0:T(128)} %eaten_in.3) | copy-start | bytes 388

commit v11 on v8

--- a/solution.py
+++ b/solution.py
@@ -256,6 +256,10 @@
     last_core = a * cores + cores - 1
     late = b == cores - 1
     barrier = pltpu.get_barrier_semaphore()
+    for place in (up, down):
+        pl.semaphore_signal(
+            barrier, inc=1, device_id={"tile": place, "tracer": last_core}, device_id_type=MESH
+        )
     if cores > 1:
         @pl.when(jnp.logical_not(late))
         def _():
@@ -264,10 +268,6 @@
                     barrier, inc=1, device_id={"tracer": target(s)}, device_id_type=MESH
                 )
             pl.semaphore_signal(barrier, inc=1, device_id={"tracer": last_core}, device_id_type=MESH)
-    for place in (up, down):
-        pl.semaphore_signal(
-            barrier, inc=1, device_id={"tile": place, "tracer": last_core}, device_id_type=MESH
-        )
     for s in range(cores - 1, cross, cores):
         pl.semaphore_signal(barrier, inc=1, device_id={"tracer": target(s)}, device_id_type=MESH)
 

time: 52.8 us -> 52.9 us (level)
  no operation moved by 1% of the time
where the time goes in v11:
time: 52.9 us; the launch traced here: 52.7 us
  Pallas kernels  52 us (98%)
  between operations  0.69 us (1%)
    pallas_call x1, Pallas kernels, on_device(): pl.pallas_call(functools.partial(transport_kernel, tiles, ranks, cores, q...  49.8 us
    pallas_call x1, Pallas kernels, on_device(): pl.pallas_call(functools.partial(finish_kernel, nl, q), out_shape=(jax.Sh...  2.2 us

profile of v11, /device:TPU:0, one launch (start us, length us, event | category | flops | bytes accessed | tf_op | source)
XLA Modules:
  0.0 52.7 jit_solution(143682311462443000)
XLA Ops:
  0.6 0.0 copy-start.2
  0.6 0.0 copy-start.1
  0.7 0.0 copy-start
  0.7 49.8 %transport.1 = (f32[32,8,32,128]{3,2,1,0:T(8,128)S(1)}, f32[2,8,32,128]{3,2,1,0:T(8,128)S(1)}, f32[8,32,128]{2,1,0:T(8,128)S(1)}, f32[3,32,128]{2,1,0:T(8,128)S(1)}) custom-call(f32[8,32,32,128]{3,2,1,0:T(8,128)} %sp.1, f32[2,32,32,128]{3,2,1,0:T(8,128)} %fc.1, f32[8,32,128]{2,1,0:T(8,128)} %th.1, s32[32,128]{1,0:T(8,128)} %dep.1, f32[32,128]{1,0:T(8,128)} %sun.1, ...), custom_call_target="tpu_custom_call" | custom-call | tf_op jit(solution)/shard_map/transport/pallas_call | solution.py:725
  50.5 0.0 copy-done.2
  50.5 0.0 copy-done.1
  50.5 0.0 copy-done
  50.5 2.2 %finish.1 = (f32[32,8,32,128]{3,2,1,0:T(8,128)}, f32[2,8,32,128]{3,2,1,0:T(8,128)}, f32[8,32,128]{2,1,0:T(8,128)}) custom-call(f32[32,8,32,128]{3,2,1,0:T(8,128)S(1)} %get-tuple-element.7.cells, f32[2,8,32,128]{3,2,1,0:T(8,128)S(1)} %get-tuple-element.8.vel, f32[8,32,128]{2,1,0:T(8,128)S(1)} %get-tuple-element.9.heat, ...), custom_call_target="tpu_custom_call" | custom-call | tf_op jit(solution)/shard_map/finish/pallas_call | solution.py:769
Async XLA Ops:
  0.6 49.9 %copy-start.2 = (f32[32]{0:T(128)S(1)}, f32[32]{0:T(128)}, u32[]{:S(2)}) copy-start(f32[32]{0:T(128)} %rate_in.3) | copy-start | bytes 388
  0.6 49.9 %copy-start.1 = (f32[32]{0:T(128)S(1)}, f32[32]{0:T(128)}, u32[]{:S(2)}) copy-start(f32[32]{0:T(128)} %att_in.3) | copy-start | bytes 388
  0.7 49.9 %copy-start = (s32[32]{0:T(128)S(1)}, s32[32]{0:T(128)}, u32[]{:S(2)}) copy-start(s32[32]{0:T(128)} %eaten_in.3) | copy-start | bytes 388
